TPU v7x, 32 devices: a whole 2x2x4 slice. The times are simulated.
32 devices in a mesh: gx: 4 (over y, x), gy: 2 (over core), gz: 4 (over z).
Axes of the slice: x: 2, y: 2, z: 4, core: 2. Of those that a mesh axis runs over, the one named last changes fastest.
Arguments:
- positions: float32 [3, 4, 2, 4, 128], P(None, 'gx', 'gy', 'gz'), may hold values from 0 to 1
- basis: float32 [30, 3, 4, 2, 4, 128], P(None, None, 'gx', 'gy', 'gz'), may hold values from -10 to 10, as said below
- neighbours: int32 [4, 2, 4, 128, 128], P('gx', 'gy', 'gz'), may hold values from 0 to 511
- used_count: int32 [4, 2, 4, 128], P('gx', 'gy', 'gz'), may hold values from 42 to 128
- kinds: int32 [4, 2, 4, 128], P('gx', 'gy', 'gz'), may hold values from 0 to 1
- map_x: int32 [4, 2, 4, 2, 64], P('gx', 'gy', 'gz'), may hold values from 0 to 127
- map_y: int32 [4, 2, 4, 2, 64], P('gx', 'gy', 'gz'), may hold values from 0 to 255
- map_z: int32 [4, 2, 4, 2, 64], P('gx', 'gy', 'gz'), may hold values from 0 to 383
- table: float32 [2, 16, 100], replicated, may hold values from -6 to 6
- fit_w1: float32 [1600, 240], replicated, may hold values from -0.15625 to 0.15625
- fit_b1: float32 [240], replicated, may hold values from -3 to 3
- fit_w2: float32 [240, 240], replicated, may hold values from -0.375 to 0.375
- fit_b2: float32 [240], replicated, may hold values from -3 to 3
- fit_out: float32 [240], replicated, may hold values from -0.375 to 0.375
Outputs:
- next_vector: float32 [3, 4, 2, 4, 128], P(None, 'gx', 'gy', 'gz')
- correlations: float32 [30], replicated
- vector_norm: float32 [], replicated
Inputs may be any that keep to these rules, and one draw needn't show every extreme that they name: `basis`: entries of order one; the stored vectors' magnitude varies from brick to brick.
All inputs are finite; a program needn't handle non-finite values.
Results may differ from a plain program's by a relative error of at most 0.0003.
Values sent between devices are 32-bit elements; how exact they have to be, the bound alone decides.
A program may use at most 64 MiB of HBM per device.

v0:
```python
import functools

import jax
import jax.numpy as jnp
from jax import lax
from jax.experimental import pallas as pl
from jax.experimental.pallas import tpu as pltpu
from jax.sharding import PartitionSpec as P

F32, BF16 = jnp.float32, jnp.bfloat16
HIGHEST = lax.Precision.HIGHEST


def split(x):
    high = x.astype(BF16)
    return high, (x - high.astype(F32)).astype(BF16)


def dot_parts(left, right, dims):
    def one(a, b):
        return lax.dot_general(a, b, (dims, ((), ())), preferred_element_type=F32)

    return one(left[0], right[0]) + (one(left[0], right[1]) + one(left[1], right[0]))


def dot_full(a, b, dims):
    return lax.dot_general(a, b, (dims, ((), ())), precision=HIGHEST, preferred_element_type=F32)


def radial_parts(d, v, mask):
    q = d[0] * d[0] + d[1] * d[1] + d[2] * d[2]
    qd = 2.0 * (d[0] * v[0] + d[1] * v[1] + d[2] * v[2])
    w = 1.0 / (q + 0.01)
    decay = jnp.exp(-q) * mask
    s = decay * jnp.sqrt(w)
    u = decay * w
    s_q = -s * (1.0 + 0.5 * w)
    u_q = -u * (1.0 + w)
    shrink = 1.0 / (1.0 + s)
    t_s = shrink * shrink
    t_q = t_s * s_q
    return q, qd, w, s, u, s_q, u_q, shrink, t_s, t_q


def hvp_kernel(ext_ref, ids_ref, counts_ref, kinds_ref, table_ref, w1_ref, w2_ref, b1_ref, b2_ref, fo_ref, out_ref,
               idt, dv, pool, env, dhi, dlo, gd, genv, gp):
    width, atoms = idt.shape
    types, levels, m1 = table_ref.shape
    m2 = w1_ref.shape[1] // m1
    ext = ext_ref.shape[1]
    banks = ext // 128
    top = float(levels - 1)
    idt[...] = ids_ref[...].T
    pool[...] = jnp.zeros_like(pool)
    counts = counts_ref[...]
    kinds = kinds_ref[...]

    def used(first, rows):
        slot = lax.broadcasted_iota(jnp.int32, (rows, atoms), 0) + first
        return jnp.where(slot < counts, 1.0, 0.0).astype(F32)

    def forward(c, carry):
        first = pl.multiple_of(c * 8, 8)
        idx = idt[pl.ds(first, 8), :]
        lane = jnp.bitwise_and(idx, 127)
        bank = jnp.right_shift(idx, 7)
        fields = []
        for f in range(6):
            got = None
            for b in range(banks):
                row = jnp.broadcast_to(ext_ref[f : f + 1, b * 128 : (b + 1) * 128], (8, 128))
                part = jnp.take_along_axis(row, lane, axis=1, mode="promise_in_bounds")
                got = part if got is None else jnp.where(bank == b, part, got)
            got = got - ext_ref[f : f + 1, :atoms]
            dv[f, pl.ds(first, 8), :] = got
            fields.append(got)
        d, v = fields[:3], fields[3:]
        _, qd, _, s, u, s_q, u_q, shrink, _, t_q = radial_parts(d, v, used(first, 8))
        scaled = s * shrink * top
        r = [s] + [u * e for e in d]
        dr = [s_q * qd] + [u_q * qd * d[e] + u * v[e] for e in range(3)]
        slope = -2.0 * top * t_q * qd
        tr = [slope * e for e in r]
        for k in range(levels):
            y = scaled - float(k)
            phi = jnp.exp(-(y * y))
            psi = y * phi
            for a in range(4):
                pool[a, k] += phi * r[a]
                pool[4 + a, k] += phi * dr[a] + psi * tr[a]
        return carry

    lax.fori_loop(0, width // 8, forward, 0)
    pooled = jnp.concatenate([jnp.sum(pool[a], axis=1) for a in range(8)], axis=1) / width
    kinds8 = jnp.concatenate([kinds] * 8, axis=1)
    chosen = None
    for t in range(types):
        part = dot_full(table_ref[t], pooled, ((0,), (0,)))
        chosen = part if t == 0 else jnp.where(kinds8 == t, part, chosen)
    for a in range(8):
        env[a] = chosen[:, a * atoms : (a + 1) * atoms]
    lead = [env[a, :m2, :] for a in range(8)]

    def describe(m, carry):
        rows = [env[a, pl.ds(m, 1), :] for a in range(8)]
        plain = rows[0] * lead[0]
        moved = rows[4] * lead[0] + rows[0] * lead[4]
        for a in range(1, 4):
            plain += rows[a] * lead[a]
            moved += rows[4 + a] * lead[a] + rows[a] * lead[4 + a]
        place = pl.ds(pl.multiple_of(m * m2, m2), m2)
        for at, value in ((0, plain), (1, moved)):
            high, low = split(value)
            dhi[place, at * atoms : (at + 1) * atoms] = high
            dlo[place, at * atoms : (at + 1) * atoms] = low
        return carry

    lax.fori_loop(0, m1, describe, 0, unroll=4)
    w1 = split(w1_ref[...])
    z1 = dot_parts(w1, (dhi[...], dlo[...]), ((1,), (0,)))
    fit = b1_ref.shape[1]
    lines = jnp.concatenate([b1_ref[...], b2_ref[...], fo_ref[...], jnp.zeros((5, fit), F32)], axis=0)
    same = lax.broadcasted_iota(jnp.int32, (8, 8), 0) == lax.broadcasted_iota(jnp.int32, (8, 8), 1)
    cols = dot_full(lines, jnp.where(same, 1.0, 0.0).astype(F32), ((0,), (0,)))
    b1, b2, fo = cols[:, 0:1], cols[:, 1:2], cols[:, 2:3]
    h1 = jnp.tanh(z1[:, :atoms] + b1)
    gate1 = 1.0 - h1 * h1
    dh1 = gate1 * z1[:, atoms:]
    w2 = w2_ref[...]
    z2 = dot_full(w2, jnp.concatenate([h1, dh1], axis=1), ((0,), (0,)))
    t2 = jnp.tanh(z2[:, :atoms] + b2)
    gate2 = 1.0 - t2 * t2
    dt2 = gate2 * z2[:, atoms:]
    gz2 = jnp.concatenate([fo * gate2, fo * (-2.0 * t2 * dt2)], axis=1)
    gh = dot_full(w2, gz2, ((1,), (0,)))
    gh1 = gh[:, :atoms] + fo
    gz1 = jnp.concatenate([gh1 * gate1, gh[:, atoms:] * gate1 - 2.0 * gh1 * h1 * dh1], axis=1)
    gd[...] = dot_parts(w1, split(gz1), ((0,), (0,)))

    def describe_back(m, acc):
        place = pl.ds(pl.multiple_of(m * m2, m2), m2)
        g = gd[place, :atoms]
        dg = gd[place, atoms:]
        out = []
        for a in range(4):
            genv[a, pl.ds(m, 1), :] = jnp.sum(g * lead[a], axis=0, keepdims=True)
            genv[4 + a, pl.ds(m, 1), :] = jnp.sum(
                dg * lead[a] + g * lead[4 + a], axis=0, keepdims=True
            )
        for a in range(4):
            out.append(acc[a] + g * env[a, pl.ds(m, 1), :])
        for a in range(4):
            out.append(
                acc[4 + a]
                + dg * env[a, pl.ds(m, 1), :]
                + g * env[4 + a, pl.ds(m, 1), :]
            )
        return tuple(out)

    acc = lax.fori_loop(0, m1, describe_back, tuple(jnp.zeros((m2, atoms), F32) for _ in range(8)), unroll=2)
    for a in range(8):
        genv[a, :m2, :] += acc[a]
    total = None
    pulled = jnp.concatenate([genv[a] for a in range(8)], axis=1)
    for t in range(types):
        part = dot_full(table_ref[t], jnp.where(kinds8 == t, pulled, 0.0), ((1,), (0,)))
        total = part if total is None else total + part
    total = total / width
    for a in range(8):
        gp[a] = total[:, a * atoms : (a + 1) * atoms]
    low_iota = lax.broadcasted_iota(jnp.int32, (128, atoms), 0)

    def backward(c, carry):
        acc, centre = carry
        first = pl.multiple_of(c * 8, 8)
        d = [dv[f, pl.ds(first, 8), :] for f in range(3)]
        v = [dv[f, pl.ds(first, 8), :] for f in range(3, 6)]
        q, qd, w, s, u, s_q, u_q, shrink, t_s, t_q = radial_parts(d, v, used(first, 8))
        s_qq = -s_q * (1.0 + 0.5 * w) + 0.5 * s * w * w
        u_qq = -u_q * (1.0 + w) + u * w * w
        t_qq = -2.0 * t_s * shrink * s_q * s_q + t_s * s_qq
        scaled = s * shrink * top
        zero = jnp.zeros((8, atoms), F32)
        s0, s1, s2, e0, e1 = ([zero] * 4 for _ in range(5))
        for k in range(levels):
            y = scaled - float(k)
            phi = jnp.exp(-(y * y))
            psi = y * phi
            chi = y * psi
            for a in range(4):
                g = gp[a, k : k + 1, :]
                h = gp[4 + a, k : k + 1, :]
                s0[a] = s0[a] + g * phi
                s1[a] = s1[a] + g * psi
                s2[a] = s2[a] + g * chi
                e0[a] = e0[a] + h * phi
                e1[a] = e1[a] + h * psi
        step = t_q * qd
        val = s0
        val_t = [-2.0 * top * e for e in s1]
        val_tt = [top * top * (4.0 * s2[a] - 2.0 * s0[a]) for a in range(4)]
        dval = [e0[a] + val_t[a] * step for a in range(4)]
        dval_t = [-2.0 * top * e1[a] + val_tt[a] * step for a in range(4)]
        big = val[1] * d[0] + val[2] * d[1] + val[3] * d[2]
        big_t = val_t[1] * d[0] + val_t[2] * d[1] + val_t[3] * d[2]
        dbig = sum(dval[1 + e] * d[e] + val[1 + e] * v[e] for e in range(3))
        dbig_t = sum(dval_t[1 + e] * d[e] + val_t[1 + e] * v[e] for e in range(3))
        kern = t_q * (val_t[0] * s + big_t * u) + val[0] * s_q + big * u_q
        dkern = (
            t_q * (dval_t[0] * s + dbig_t * u)
            + dval[0] * s_q
            + dbig * u_q
            + qd * (
                t_qq * (val_t[0] * s + big_t * u)
                + t_q * (val_t[0] * s_q + big_t * u_q)
                + val[0] * s_qq
                + big * u_qq
            )
        )
        du = u_q * qd
        force = [2.0 * (v[e] * kern + d[e] * dkern) + du * val[1 + e] + u * dval[1 + e] for e in range(3)]
        centre = tuple(centre[e] - force[e] for e in range(3))
        idx = idt[pl.ds(first, 8), :]
        lane = jnp.bitwise_and(idx, 127)
        bank = jnp.right_shift(idx, 7)
        rows = []
        for e in range(3):
            high = force[e].astype(BF16).astype(F32)
            for part in (high, force[e] - high):
                for b in range(banks):
                    rows.append(jnp.where(bank == b, part, 0.0))
        lefts, rights = [], []
        for r in range(8):
            lefts.append(jnp.concatenate([x[r : r + 1, :] for x in rows], axis=0).astype(BF16))
            rights.append(jnp.where(lane[r : r + 1, :] == low_iota, 1.0, 0.0).astype(BF16))
        acc = acc + lax.dot_general(
            jnp.concatenate(lefts, axis=1),
            jnp.concatenate(rights, axis=1),
            (((1,), (1,)), ((), ())),
            preferred_element_type=F32,
        )
        return acc, centre

    out_ref[...] = jnp.zeros_like(out_ref)
    start = (jnp.zeros((6 * banks, 128), F32), tuple(jnp.zeros((8, atoms), F32) for _ in range(3)))
    acc, centre = lax.fori_loop(0, width // 8, backward, start)
    for e in range(3):
        base = 2 * banks * e
        for b in range(banks):
            row = acc[base + b : base + b + 1] + acc[base + banks + b : base + banks + b + 1]
            if b == 0:
                row = row + jnp.sum(centre[e], axis=0, keepdims=True)
            out_ref[e : e + 1, b * 128 : (b + 1) * 128] = row


def device_hvp(fields, neighbour_ids, counts, species, table, w1, w2, b1, b2, fo):
    atoms, width = neighbour_ids.shape
    types, levels, m1 = table.shape
    ext = fields.shape[1]
    m2 = w1.shape[1] // m1
    vmem = pl.BlockSpec(memory_space=pltpu.VMEM)
    return pl.pallas_call(
        hvp_kernel,
        out_shape=jax.ShapeDtypeStruct((8, ext), F32),
        in_specs=[vmem] * 10,
        out_specs=vmem,
        scratch_shapes=[
            pltpu.VMEM((width, atoms), jnp.int32),
            pltpu.VMEM((6, width, atoms), F32),
            pltpu.VMEM((8, levels, 8, atoms), F32),
            pltpu.VMEM((8, m1, atoms), F32),
            pltpu.VMEM((m1 * m2, 2 * atoms), BF16),
            pltpu.VMEM((m1 * m2, 2 * atoms), BF16),
            pltpu.VMEM((m1 * m2, 2 * atoms), F32),
            pltpu.VMEM((8, m1, atoms), F32),
            pltpu.VMEM((8, levels, atoms), F32),
        ],
        compiler_params=pltpu.CompilerParams(vmem_limit_bytes=48 << 20),
        cost_estimate=pl.CostEstimate(flops=1000000000, bytes_accessed=4000000, transcendentals=600000),
        name="hvp",
    )(fields, neighbour_ids, counts.reshape(1, atoms), species.reshape(1, atoms), table, w1, w2, b1[None], b2[None], fo[None])


AXES = ("gx", "gy", "gz")
MESH = pl.DeviceIdType.MESH


def beside(axis):
    peers = lax.axis_size(axis)
    me = lax.axis_index(axis)
    return lax.rem(me + peers - 1, peers), lax.rem(me + 1, peers)


def greet(partners):
    barrier = pltpu.get_barrier_semaphore()
    for axis, peer in partners:
        pl.semaphore_signal(barrier, inc=1, device_id={axis: peer}, device_id_type=MESH)
    return lambda: pl.semaphore_wait(barrier, len(partners))


def three_parts(x):
    high = x.astype(BF16)
    rest = x - high.astype(F32)
    middle = rest.astype(BF16)
    low = (rest - middle.astype(F32)).astype(BF16)
    return jnp.concatenate([high.astype(F32), middle.astype(F32), low.astype(F32)], axis=0).astype(BF16)


def select_dot(x, onehot, dims):
    n = x.shape[0]
    out = lax.dot_general(three_parts(x), onehot, (dims, ((), ())), preferred_element_type=F32)
    return (out[:n] + out[n : 2 * n]) + out[2 * n :]


def exchange(axis, section, source, landed, send_sem, recv_sem):
    lower, upper = beside(axis)
    copies = []
    for way, peer in ((0, upper), (1, lower)):
        copy = pltpu.make_async_remote_copy(
            src_ref=source,
            dst_ref=landed.at[section, way],
            send_sem=send_sem.at[section, way],
            recv_sem=recv_sem.at[section, way],
            device_id={axis: peer},
            device_id_type=MESH,
        )
        copy.start()
        copies.append(copy)
    for copy in copies:
        copy.wait_recv()
    return copies


def chosen_columns(map_ref, columns):
    map_row = jnp.concatenate([map_ref[1:2, :], map_ref[0:1, :]], axis=1)
    rows = lax.broadcasted_iota(jnp.int32, (columns, map_row.shape[1]), 0)
    return jnp.where(rows == map_row, 1.0, 0.0).astype(BF16)


def halo_kernel(places_ref, basis_ref, map_x_ref, map_y_ref, map_z_ref, out_ref,
                sent, landed, send_sem, recv_sem):
    atoms = places_ref.shape[2]
    maps = (map_x_ref, map_y_ref, map_z_ref)
    pair = 2 * map_x_ref.shape[1]
    arrived = greet([(axis, peer) for axis in AXES for peer in beside(axis)])
    last = basis_ref.shape[0] - 1
    for c in range(3):
        out_ref[c : c + 1, :atoms] = places_ref[c]
        out_ref[3 + c : 4 + c, :atoms] = basis_ref[last, c]
    out_ref[6:8, :] = jnp.zeros((2, out_ref.shape[1]), F32)
    lane = lax.broadcasted_iota(jnp.int32, (8, pair), 1)
    row = lax.broadcasted_iota(jnp.int32, (8, pair), 0)
    early = lane < pair // 2
    waiting = []
    onehots = [chosen_columns(maps[section], atoms + section * pair) for section in range(3)]
    for section, axis in enumerate(AXES):
        current = atoms + section * pair
        sent[section] = select_dot(out_ref[:, :current], onehots[section], ((1,), (0,)))
        if section == 0:
            arrived()
        waiting += exchange(axis, section, sent.at[section], landed, send_sem, recv_sem)
        shift = jnp.where(row == section, jnp.where(early, -1.0, 1.0), 0.0)
        fresh = jnp.where(early, landed[section, 0], landed[section, 1]) + shift
        out_ref[:, current : current + pair] = fresh
    for copy in waiting:
        copy.wait_send()


def finish_kernel(w_ref, map_x_ref, map_y_ref, map_z_ref, basis_ref, next_ref, corr_ref, norm_ref,
                  work, landed, stack, parts, send_sem, recv_sem, sum_send, sum_recv):
    stored = basis_ref.shape[0]
    rows = stack.shape[0]
    atoms = basis_ref.shape[3]
    maps = (map_x_ref, map_y_ref, map_z_ref)
    pair = 2 * map_x_ref.shape[1]
    sizes = [lax.axis_size(axis) for axis in AXES]
    entries = 3 * atoms * sizes[0] * sizes[1] * sizes[2]
    partners = []
    for axis, peers in zip(AXES, sizes):
        me = lax.axis_index(axis)
        partners += [(axis, lax.rem(me + step, peers)) for step in range(1, peers)]
    arrived = greet(partners)
    early = lax.broadcasted_iota(jnp.int32, (8, pair), 1) < pair // 2
    work[...] = w_ref[...]
    stack[...] = jnp.zeros_like(stack)
    for k in range(stored):
        for c in range(3):
            stack[k : k + 1, c * atoms : (c + 1) * atoms] = basis_ref[k, c]
    waiting = []
    onehots = [chosen_columns(maps[section], atoms + section * pair) for section in range(3)]
    arrived()
    for section in (2, 1, 0):
        current = atoms + section * pair
        source = w_ref if section == 2 else work
        waiting += exchange(
            AXES[section], section, source.at[:, current : current + pair], landed, send_sem, recv_sem
        )
        back = jnp.where(early, landed[section, 1], landed[section, 0])
        work[:, :current] = work[:, :current] + select_dot(back, onehots[section], ((1,), (1,)))
    hv = [work[c : c + 1, :atoms] for c in range(3)]
    for c in range(3):
        stack[stored : stored + 1, c * atoms : (c + 1) * atoms] = hv[c]
    local = dot_full(stack[...], stack[...], ((1,), (1,)))
    local = jnp.concatenate([local[r : r + 8] for r in range(0, rows, 8)], axis=1)
    base = 0
    for at, (axis, peers) in enumerate(zip(AXES, sizes)):
        me = lax.axis_index(axis)
        parts[base + me] = local
        copies = []
        for step in range(1, peers):
            copy = pltpu.make_async_remote_copy(
                src_ref=parts.at[base + me],
                dst_ref=parts.at[base + me],
                send_sem=sum_send.at[base + step],
                recv_sem=sum_recv.at[base + step],
                device_id={axis: lax.rem(me + step, peers)},
                device_id_type=MESH,
            )
            copy.start()
            copies.append(copy)
        for copy in copies:
            copy.wait_recv()
        waiting += copies
        local = parts[base]
        for other in range(1, peers):
            local = local + parts[base + other]
        base += peers
    for copy in waiting:
        copy.wait_send()
    local = jnp.concatenate([local[:, r : r + rows] for r in range(0, rows * rows // 8, rows)], axis=0) / entries
    in_row = lax.broadcasted_iota(jnp.int32, (rows, rows), 0)
    in_col = lax.broadcasted_iota(jnp.int32, (rows, rows), 1)
    kept = jnp.logical_and(in_row < stored, in_col < stored)
    column = jnp.where(in_row[:, 0:1] < stored, local[:, stored : stored + 1], 0.0)
    line = local[stored : stored + 1, :]
    line_kept = jnp.where(in_col[0:1] < stored, line, 0.0)
    quad = jnp.where(kept, local * column * line_kept, 0.0)

    def add_up(x):
        return jnp.sum(jnp.sum(x, axis=1, keepdims=True), axis=0, keepdims=True)

    plain = local[stored : stored + 1, stored : stored + 1]
    square = plain - 2.0 * add_up(line_kept * line_kept) + add_up(quad)
    norm = jnp.sqrt(square + 1e-06)
    norm_ref[...] = norm
    corr_ref[...] = line[:, :stored]
    for c in range(3):
        projected = jnp.sum(column * stack[:, c * atoms : (c + 1) * atoms], axis=0, keepdims=True)
        next_ref[c] = (hv[c] - projected) / norm


def on_device(positions, basis, neighbours, used_count, kinds, map_x, map_y, map_z,
              table, fit_w1, fit_b1, fit_w2, fit_b2, fit_out):
    atoms = positions.shape[-1]
    stored = basis.shape[0]
    pair = 2 * map_x.shape[-1]
    ext = atoms + 3 * pair
    vectors = basis.reshape(stored, 3, 1, atoms)
    maps = tuple(m.reshape(2, -1) for m in (map_x, map_y, map_z))
    vmem = pl.BlockSpec(memory_space=pltpu.VMEM)
    fields = pl.pallas_call(
        halo_kernel,
        out_shape=jax.ShapeDtypeStruct((8, ext), F32),
        in_specs=[vmem] * 5,
        out_specs=vmem,
        scratch_shapes=[
            pltpu.VMEM((3, 8, pair), F32),
            pltpu.VMEM((3, 2, 8, pair), F32),
            pltpu.SemaphoreType.DMA((3, 2)),
            pltpu.SemaphoreType.DMA((3, 2)),
        ],
        compiler_params=pltpu.CompilerParams(collective_id=0, has_side_effects=True),
        cost_estimate=pl.CostEstimate(flops=1000000000, bytes_accessed=4000000, transcendentals=0),
        name="halo",
    )(positions.reshape(3, 1, atoms), vectors, *maps)
    products = device_hvp(
        fields,
        neighbours.reshape(atoms, -1),
        used_count.reshape(atoms),
        kinds.reshape(atoms),
        table,
        fit_w1.T,
        fit_w2,
        fit_b1,
        fit_b2,
        fit_out,
    )
    rows = (stored + 8) // 8 * 8
    slots = sum(lax.axis_size(axis) for axis in AXES)
    next_vector, correlations, norm = pl.pallas_call(
        finish_kernel,
        out_shape=(
            jax.ShapeDtypeStruct((3, 1, atoms), F32),
            jax.ShapeDtypeStruct((1, stored), F32),
            jax.ShapeDtypeStruct((1, 1), F32),
        ),
        in_specs=[vmem] * 5,
        out_specs=(vmem,) * 3,
        scratch_shapes=[
            pltpu.VMEM((8, ext), F32),
            pltpu.VMEM((3, 2, 8, pair), F32),
            pltpu.VMEM((rows, 3 * atoms), F32),
            pltpu.VMEM((slots, 8, rows * rows // 8), F32),
            pltpu.SemaphoreType.DMA((3, 2)),
            pltpu.SemaphoreType.DMA((3, 2)),
            pltpu.SemaphoreType.DMA((slots,)),
            pltpu.SemaphoreType.DMA((slots,)),
        ],
        compiler_params=pltpu.CompilerParams(collective_id=1, has_side_effects=True),
        name="finish",
    )(products, *maps, vectors)
    return next_vector.reshape(positions.shape), correlations.reshape(stored), norm.reshape(())


def solution(mesh):
    placed = (
        P(None, "gx", "gy", "gz", None),
        P(None, None, "gx", "gy", "gz", None),
        P("gx", "gy", "gz", None, None),
        P("gx", "gy", "gz", None),
        P("gx", "gy", "gz", None),
        P("gx", "gy", "gz", None, None),
        P("gx", "gy", "gz", None, None),
        P("gx", "gy", "gz", None, None),
        P(),
        P(),
        P(),
        P(),
        P(),
        P(),
    )
    return jax.shard_map(
        on_device,
        mesh=mesh,
        in_specs=placed,
        out_specs=(P(None, "gx", "gy", "gz", None), P(), P()),
        check_vma=False,
    )
```

profile of v0, /device:TPU:0, one launch (start us, length us, event | category | flops | bytes accessed | tf_op | source)
XLA Modules:
  0.0 56.6 jit_solution(1200142199646701598)
XLA Ops:
  0.6 0.0 copy-start.1
  0.6 0.0 copy-start.2
  0.7 0.0 copy-start.3
  0.7 0.0 copy-start.4
  0.7 0.0 copy-start.5
  0.7 0.0 copy-start.6
  0.7 0.0 copy-start.7
  0.7 0.0 copy-start.8
  0.7 0.0 copy-start.9
  0.7 13.2 %halo.1.ext_ref = f32[8,512]{1,0:T(8,128)} custom-call(f32[3,1,128]{2,1,0:T(1,128)} %bitcast.33, f32[30,3,1,128]{3,2,1,0:T(1,128)} %bitcast.24, s32[2,64]{1,0:T(2,128)} %bitcast.27, s32[2,64]{1,0:T(2,128)} %bitcast.29, s32[2,64]{1,0:T(2,128)} %bitcast.31), custom_call_target="tpu_custom_call" | custom-call | flops 1000000000 | bytes 4000000 | tf_op jit(solution)/shard_map/halo/pallas_call | solution.py:461
  14.0 0.0 copy-done.1
  14.0 0.0 copy-done.2
  14.0 0.0 copy-done.3
  14.0 0.0 copy-done.4
  14.0 0.0 copy-done.5
  14.0 0.0 copy-done.6
  14.0 0.0 copy-done.7
  14.0 0.0 copy-done.8
  14.0 0.0 copy-done.9
  14.0 0.0 copy-start.10
  14.1 0.7 %copy-done.10 = f32[8,512]{1,0:T(8,128)S(1)} copy-done((f32[8,512]{1,0:T(8,128)S(1)}, f32[8,512]{1,0:T(8,128)}, u32[]{:S(2)}) %copy-start.10) | copy-done | bytes 16408
  14.8 17.9 %hvp.1.w_ref = f32[8,512]{1,0:T(8,128)S(1)} custom-call(f32[8,512]{1,0:T(8,128)S(1)} %copy-done.10, s32[128,128]{1,0:T(8,128)S(1)} %bitcast.18, s32[1,128]{1,0:T(1,128)S(1)} %bitcast.22, s32[1,128]{1,0:T(1,128)S(1)} %bitcast.23, f32[2,16,100]{2,1,0:T(8,128)S(1)} %copy-done.4, f32[240,1600]{1,0:T(8,128)S(1)} %bitcast.17, f32[240,240]{1,0:T(8,128)S(1)} %copy-done.2, ...), custom_call_target="tpu_custom_call" | custom-call | flops 1000000000 | bytes 4000000 | tf_op jit(solution)/shard_map/hvp/pallas_call | solution.py:262
  32.7 0.0 copy-start
  32.7 0.6 %copy-done = f32[8,512]{1,0:T(8,128)} copy-done((f32[8,512]{1,0:T(8,128)}, f32[8,512]{1,0:T(8,128)S(1)}, u32[]{:S(2)}) %copy-start) | copy-done | bytes 16408
  33.3 19.3 %finish.1 = (f32[3,1,128]{2,1,0:T(1,128)}, f32[1,30]{1,0:T(1,128)}, f32[1,1]{1,0:T(1,128)}) custom-call(f32[8,512]{1,0:T(8,128)} %copy-done, s32[2,64]{1,0:T(2,128)} %bitcast.28, s32[2,64]{1,0:T(2,128)} %bitcast.30, s32[2,64]{1,0:T(2,128)} %bitcast.32, f32[30,3,1,128]{3,2,1,0:T(1,128)} %bitcast.25), custom_call_target="tpu_custom_call" | custom-call | tf_op jit(solution)/shard_map/finish/pallas_call | solution.py:490
  52.5 1.2 %copy.21 = f32[3,1,1,1,128]{4,3,2,1,0:T(1,128)} copy(f32[3,1,1,1,128]{4,3,2,1,0:T(1,128)} %bitcast.26) | data formatting | bytes 3072
  53.8 1.1 %copy.22 = f32[30]{0:T(128)} copy(f32[30]{0:T(128)} %bitcast.34) | data formatting | bytes 240
Async XLA Ops:
  0.6 13.3 %copy-start.1 = (f32[1600,240]{0,1:T(8,128)S(1)}, f32[1600,240]{0,1:T(8,128)}, u32[]{:S(2)}) copy-start(f32[1600,240]{0,1:T(8,128)} %param.23) | copy-start | bytes 4608004
  0.6 13.3 %copy-start.2 = (f32[240,240]{1,0:T(8,128)S(1)}, f32[240,240]{1,0:T(8,128)}, u32[]{:S(2)}) copy-start(f32[240,240]{1,0:T(8,128)} %w2_ref.1) | copy-start | bytes 691204
  0.7 13.3 %copy-start.3 = (s32[1,1,1,128,128]{4,3,2,1,0:T(8,128)S(1)}, s32[1,1,1,128,128]{4,3,2,1,0:T(8,128)}, u32[]{:S(2)}) copy-start(s32[1,1,1,128,128]{4,3,2,1,0:T(8,128)} %param.16) | copy-start | bytes 196612
  0.7 13.3 %copy-start.4 = (f32[2,16,100]{2,1,0:T(8,128)S(1)}, f32[2,16,100]{2,1,0:T(8,128)}, u32[]{:S(2)}) copy-start(f32[2,16,100]{2,1,0:T(8,128)} %table_ref.1) | copy-start | bytes 38404
  0.7 13.3 %copy-start.5 = (f32[240]{0:T(256)S(1)}, f32[240]{0:T(256)}, u32[]{:S(2)}) copy-start(f32[240]{0:T(256)} %param.24) | copy-start | bytes 2884
  0.7 13.3 %copy-start.6 = (f32[240]{0:T(256)S(1)}, f32[240]{0:T(256)}, u32[]{:S(2)}) copy-start(f32[240]{0:T(256)} %param.26) | copy-start | bytes 2884
  0.7 13.3 %copy-start.7 = (f32[240]{0:T(256)S(1)}, f32[240]{0:T(256)}, u32[]{:S(2)}) copy-start(f32[240]{0:T(256)} %param.27) | copy-start | bytes 2884
  0.7 13.3 %copy-start.8 = (s32[1,1,1,128]{3,2,1,0:T(1,128)S(1)}, s32[1,1,1,128]{3,2,1,0:T(1,128)}, u32[]{:S(2)}) copy-start(s32[1,1,1,128]{3,2,1,0:T(1,128)} %param.17) | copy-start | bytes 1540
  0.7 13.3 %copy-start.9 = (s32[1,1,1,128]{3,2,1,0:T(1,128)S(1)}, s32[1,1,1,128]{3,2,1,0:T(1,128)}, u32[]{:S(2)}) copy-start(s32[1,1,1,128]{3,2,1,0:T(1,128)} %param.18) | copy-start | bytes 1540
  14.0 0.7 %copy-start.10 = (f32[8,512]{1,0:T(8,128)S(1)}, f32[8,512]{1,0:T(8,128)}, u32[]{:S(2)}) copy-start(f32[8,512]{1,0:T(8,128)} %halo.1.ext_ref) | copy-start | bytes 49156
  32.7 0.6 %copy-start = (f32[8,512]{1,0:T(8,128)}, f32[8,512]{1,0:T(8,128)S(1)}, u32[]{:S(2)}) copy-start(f32[8,512]{1,0:T(8,128)S(1)} %hvp.1.w_ref) | copy-start | bytes 49156
where the time goes:
time: 56.9 us; the launch traced here: 56.6 us
  Pallas kernels  50.4 us (89%)
  local copies, waits for them, and re-layouts  3.68 us (6%)
  between operations  2.58 us (5%)
    pallas_call x1, Pallas kernels, on_device(): pl.pallas_call(finish_kernel, out_shape=(jax.ShapeDtypeStruct((3, 1, atom...  19.3 us
    pallas_call x1, Pallas kernels, device_hvp(): pl.pallas_call(hvp_kernel, out_shape=jax.ShapeDtypeStruct((8, ext), F32),...  17.9 us
    pallas_call x1, Pallas kernels, on_device(): pl.pallas_call(halo_kernel, out_shape=jax.ShapeDtypeStruct((8, ext), F32)...  13.2 us
    unnamed x24, local copies, waits for them, and re-layouts  3.68 us

commit v1 on v0

v1 whole, which is shorter than its diff:
```python
import functools

import jax
import jax.numpy as jnp
from jax import lax
from jax.experimental import pallas as pl
from jax.experimental.pallas import tpu as pltpu
from jax.sharding import PartitionSpec as P

F32, BF16 = jnp.float32, jnp.bfloat16
HIGHEST = lax.Precision.HIGHEST


def split(x):
    high = x.astype(BF16)
    return high, (x - high.astype(F32)).astype(BF16)


def dot_parts(left, right, dims):
    def one(a, b):
        return lax.dot_general(a, b, (dims, ((), ())), preferred_element_type=F32)

    return one(left[0], right[0]) + (one(left[0], right[1]) + one(left[1], right[0]))


def dot_full(a, b, dims):
    return lax.dot_general(a, b, (dims, ((), ())), precision=HIGHEST, preferred_element_type=F32)


def radial_parts(d, v, mask):
    q = d[0] * d[0] + d[1] * d[1] + d[2] * d[2]
    qd = 2.0 * (d[0] * v[0] + d[1] * v[1] + d[2] * v[2])
    w = 1.0 / (q + 0.01)
    decay = jnp.exp(-q) * mask
    s = decay * jnp.sqrt(w)
    u = decay * w
    s_q = -s * (1.0 + 0.5 * w)
    u_q = -u * (1.0 + w)
    shrink = 1.0 / (1.0 + s)
    t_s = shrink * shrink
    t_q = t_s * s_q
    return q, qd, w, s, u, s_q, u_q, shrink, t_s, t_q


def hessian_product(ext_ref, idt, counts_ref, kinds_ref, table_ref, w1_ref, w2_ref, b1_ref, b2_ref, fo_ref, out_ref,
                    dv, pool, env, dhi, dlo, gd, genv, gp):
    width, atoms = idt.shape
    types, levels, m1 = table_ref.shape
    m2 = w1_ref.shape[1] // m1
    ext = ext_ref.shape[1]
    banks = ext // 128
    top = float(levels - 1)
    pool[...] = jnp.zeros_like(pool)
    counts = counts_ref[...]
    kinds = kinds_ref[...]

    def used(first, rows):
        slot = lax.broadcasted_iota(jnp.int32, (rows, atoms), 0) + first
        return jnp.where(slot < counts, 1.0, 0.0).astype(F32)

    def forward(c, carry):
        first = pl.multiple_of(c * 8, 8)
        idx = idt[pl.ds(first, 8), :]
        lane = jnp.bitwise_and(idx, 127)
        bank = jnp.right_shift(idx, 7)
        fields = []
        for f in range(6):
            got = None
            for b in range(banks):
                row = jnp.broadcast_to(ext_ref[f : f + 1, b * 128 : (b + 1) * 128], (8, 128))
                part = jnp.take_along_axis(row, lane, axis=1, mode="promise_in_bounds")
                got = part if got is None else jnp.where(bank == b, part, got)
            got = got - ext_ref[f : f + 1, :atoms]
            dv[f, pl.ds(first, 8), :] = got
            fields.append(got)
        d, v = fields[:3], fields[3:]
        _, qd, _, s, u, s_q, u_q, shrink, _, t_q = radial_parts(d, v, used(first, 8))
        scaled = s * shrink * top
        r = [s] + [u * e for e in d]
        dr = [s_q * qd] + [u_q * qd * d[e] + u * v[e] for e in range(3)]
        slope = -2.0 * top * t_q * qd
        tr = [slope * e for e in r]
        for k in range(levels):
            y = scaled - float(k)
            phi = jnp.exp(-(y * y))
            psi = y * phi
            for a in range(4):
                pool[a, k] += phi * r[a]
                pool[4 + a, k] += phi * dr[a] + psi * tr[a]
        return carry

    lax.fori_loop(0, width // 8, forward, 0)
    pooled = jnp.concatenate([jnp.sum(pool[a], axis=1) for a in range(8)], axis=1) / width
    kinds8 = jnp.concatenate([kinds] * 8, axis=1)
    chosen = None
    for t in range(types):
        part = dot_full(table_ref[t], pooled, ((0,), (0,)))
        chosen = part if t == 0 else jnp.where(kinds8 == t, part, chosen)
    for a in range(8):
        env[a] = chosen[:, a * atoms : (a + 1) * atoms]
    lead = [env[a, :m2, :] for a in range(8)]

    def describe(m, carry):
        rows = [env[a, pl.ds(m, 1), :] for a in range(8)]
        plain = rows[0] * lead[0]
        moved = rows[4] * lead[0] + rows[0] * lead[4]
        for a in range(1, 4):
            plain += rows[a] * lead[a]
            moved += rows[4 + a] * lead[a] + rows[a] * lead[4 + a]
        place = pl.ds(pl.multiple_of(m * m2, m2), m2)
        for at, value in ((0, plain), (1, moved)):
            high, low = split(value)
            dhi[place, at * atoms : (at + 1) * atoms] = high
            dlo[place, at * atoms : (at + 1) * atoms] = low
        return carry

    lax.fori_loop(0, m1, describe, 0, unroll=4)
    w1 = split(w1_ref[...])
    z1 = dot_parts(w1, (dhi[...], dlo[...]), ((1,), (0,)))
    fit = b1_ref.shape[1]
    lines = jnp.concatenate([b1_ref[...], b2_ref[...], fo_ref[...], jnp.zeros((5, fit), F32)], axis=0)
    same = lax.broadcasted_iota(jnp.int32, (8, 8), 0) == lax.broadcasted_iota(jnp.int32, (8, 8), 1)
    cols = dot_full(lines, jnp.where(same, 1.0, 0.0).astype(F32), ((0,), (0,)))
    b1, b2, fo = cols[:, 0:1], cols[:, 1:2], cols[:, 2:3]
    h1 = jnp.tanh(z1[:, :atoms] + b1)
    gate1 = 1.0 - h1 * h1
    dh1 = gate1 * z1[:, atoms:]
    w2 = w2_ref[...]
    z2 = dot_full(w2, jnp.concatenate([h1, dh1], axis=1), ((0,), (0,)))
    t2 = jnp.tanh(z2[:, :atoms] + b2)
    gate2 = 1.0 - t2 * t2
    dt2 = gate2 * z2[:, atoms:]
    gz2 = jnp.concatenate([fo * gate2, fo * (-2.0 * t2 * dt2)], axis=1)
    gh = dot_full(w2, gz2, ((1,), (0,)))
    gh1 = gh[:, :atoms] + fo
    gz1 = jnp.concatenate([gh1 * gate1, gh[:, atoms:] * gate1 - 2.0 * gh1 * h1 * dh1], axis=1)
    gd[...] = dot_parts(w1, split(gz1), ((0,), (0,)))

    def describe_back(m, acc):
        place = pl.ds(pl.multiple_of(m * m2, m2), m2)
        g = gd[place, :atoms]
        dg = gd[place, atoms:]
        out = []
        for a in range(4):
            genv[a, pl.ds(m, 1), :] = jnp.sum(g * lead[a], axis=0, keepdims=True)
            genv[4 + a, pl.ds(m, 1), :] = jnp.sum(
                dg * lead[a] + g * lead[4 + a], axis=0, keepdims=True
            )
        for a in range(4):
            out.append(acc[a] + g * env[a, pl.ds(m, 1), :])
        for a in range(4):
            out.append(
                acc[4 + a]
                + dg * env[a, pl.ds(m, 1), :]
                + g * env[4 + a, pl.ds(m, 1), :]
            )
        return tuple(out)

    acc = lax.fori_loop(0, m1, describe_back, tuple(jnp.zeros((m2, atoms), F32) for _ in range(8)), unroll=2)
    for a in range(8):
        genv[a, :m2, :] += acc[a]
    total = None
    pulled = jnp.concatenate([genv[a] for a in range(8)], axis=1)
    for t in range(types):
        part = dot_full(table_ref[t], jnp.where(kinds8 == t, pulled, 0.0), ((1,), (0,)))
        total = part if total is None else total + part
    total = total / width
    for a in range(8):
        gp[a] = total[:, a * atoms : (a + 1) * atoms]
    low_iota = lax.broadcasted_iota(jnp.int32, (128, atoms), 0)

    def backward(c, carry):
        acc, centre = carry
        first = pl.multiple_of(c * 8, 8)
        d = [dv[f, pl.ds(first, 8), :] for f in range(3)]
        v = [dv[f, pl.ds(first, 8), :] for f in range(3, 6)]
        q, qd, w, s, u, s_q, u_q, shrink, t_s, t_q = radial_parts(d, v, used(first, 8))
        s_qq = -s_q * (1.0 + 0.5 * w) + 0.5 * s * w * w
        u_qq = -u_q * (1.0 + w) + u * w * w
        t_qq = -2.0 * t_s * shrink * s_q * s_q + t_s * s_qq
        scaled = s * shrink * top
        zero = jnp.zeros((8, atoms), F32)
        s0, s1, s2, e0, e1 = ([zero] * 4 for _ in range(5))
        for k in range(levels):
            y = scaled - float(k)
            phi = jnp.exp(-(y * y))
            psi = y * phi
            chi = y * psi
            for a in range(4):
                g = gp[a, k : k + 1, :]
                h = gp[4 + a, k : k + 1, :]
                s0[a] = s0[a] + g * phi
                s1[a] = s1[a] + g * psi
                s2[a] = s2[a] + g * chi
                e0[a] = e0[a] + h * phi
                e1[a] = e1[a] + h * psi
        step = t_q * qd
        val = s0
        val_t = [-2.0 * top * e for e in s1]
        val_tt = [top * top * (4.0 * s2[a] - 2.0 * s0[a]) for a in range(4)]
        dval = [e0[a] + val_t[a] * step for a in range(4)]
        dval_t = [-2.0 * top * e1[a] + val_tt[a] * step for a in range(4)]
        big = val[1] * d[0] + val[2] * d[1] + val[3] * d[2]
        big_t = val_t[1] * d[0] + val_t[2] * d[1] + val_t[3] * d[2]
        dbig = sum(dval[1 + e] * d[e] + val[1 + e] * v[e] for e in range(3))
        dbig_t = sum(dval_t[1 + e] * d[e] + val_t[1 + e] * v[e] for e in range(3))
        kern = t_q * (val_t[0] * s + big_t * u) + val[0] * s_q + big * u_q
        dkern = (
            t_q * (dval_t[0] * s + dbig_t * u)
            + dval[0] * s_q
            + dbig * u_q
            + qd * (
                t_qq * (val_t[0] * s + big_t * u)
                + t_q * (val_t[0] * s_q + big_t * u_q)
                + val[0] * s_qq
                + big * u_qq
            )
        )
        du = u_q * qd
        force = [2.0 * (v[e] * kern + d[e] * dkern) + du * val[1 + e] + u * dval[1 + e] for e in range(3)]
        centre = tuple(centre[e] - force[e] for e in range(3))
        idx = idt[pl.ds(first, 8), :]
        lane = jnp.bitwise_and(idx, 127)
        bank = jnp.right_shift(idx, 7)
        rows = []
        for e in range(3):
            high = force[e].astype(BF16).astype(F32)
            for part in (high, force[e] - high):
                for b in range(banks):
                    rows.append(jnp.where(bank == b, part, 0.0))
        lefts, rights = [], []
        for r in range(8):
            lefts.append(jnp.concatenate([x[r : r + 1, :] for x in rows], axis=0).astype(BF16))
            rights.append(jnp.where(lane[r : r + 1, :] == low_iota, 1.0, 0.0).astype(BF16))
        acc = acc + lax.dot_general(
            jnp.concatenate(lefts, axis=1),
            jnp.concatenate(rights, axis=1),
            (((1,), (1,)), ((), ())),
            preferred_element_type=F32,
        )
        return acc, centre

    out_ref[...] = jnp.zeros_like(out_ref)
    start = (jnp.zeros((6 * banks, 128), F32), tuple(jnp.zeros((8, atoms), F32) for _ in range(3)))
    acc, centre = lax.fori_loop(0, width // 8, backward, start)
    for e in range(3):
        base = 2 * banks * e
        for b in range(banks):
            row = acc[base + b : base + b + 1] + acc[base + banks + b : base + banks + b + 1]
            if b == 0:
                row = row + jnp.sum(centre[e], axis=0, keepdims=True)
            out_ref[e : e + 1, b * 128 : (b + 1) * 128] = row


AXES = ("gx", "gy", "gz")
MESH = pl.DeviceIdType.MESH
GROUP_LIMIT = 32


def sizes_of():
    return [lax.axis_size(axis) for axis in AXES]


def plane_offsets():
    def along(size):
        return (0, 1) if size == 2 else (0, 1, -1)

    _, ny, nz = sizes_of()
    return [(dy, dz) for dz in along(nz) for dy in along(ny)]


def device_at(shift):
    return {
        axis: lax.rem(lax.axis_index(axis) + (step + peers) % peers, peers)
        for axis, step, peers in zip(AXES, shift, sizes_of())
    }


def reduction_groups():
    sizes = sizes_of()
    groups = []
    for at in range(3):
        if groups and groups[-1][1] * sizes[at] <= GROUP_LIMIT:
            groups[-1] = (groups[-1][0] + [at], groups[-1][1] * sizes[at])
        else:
            groups.append(([at], sizes[at]))
    out = []
    for members, count in groups:
        shifts = [[0, 0, 0]]
        for at in members:
            shifts = [s[:at] + [step] + s[at + 1 :] for s in shifts for step in range(sizes[at])]
        out.append((members, count, [tuple(s) for s in shifts if any(s)]))
    return out


def place_in(members):
    sizes = sizes_of()
    me = 0
    for at in members:
        me = me * sizes[at] + lax.axis_index(AXES[at])
    return me


def three_parts(x):
    high = x.astype(BF16)
    rest = x - high.astype(F32)
    middle = rest.astype(BF16)
    low = (rest - middle.astype(F32)).astype(BF16)
    return jnp.concatenate([high.astype(F32), middle.astype(F32), low.astype(F32)], axis=0).astype(BF16)


def select_dot(x, onehot, dims):
    n = x.shape[0]
    out = lax.dot_general(three_parts(x), onehot, (dims, ((), ())), preferred_element_type=F32)
    return (out[:n] + out[n : 2 * n]) + out[2 * n :]


def chosen_columns(map_row, columns):
    rows = lax.broadcasted_iota(jnp.int32, (columns, map_row.shape[1]), 0).astype(F32)
    return jnp.where(rows == map_row, 1.0, 0.0).astype(BF16)


def sides(parts, early):
    if -1 in parts:
        return jnp.where(early, parts[-1], parts[1])
    return parts[1]


def one_side(x, step, distinct, early):
    if not distinct:
        return x
    return jnp.where(early, x, 0.0) if step == -1 else jnp.where(early, 0.0, x)


class Sender:
    def __init__(self, send_sem, recv_sem):
        self.send_sem, self.recv_sem, self.used, self.started = send_sem, recv_sem, 0, []

    def send(self, source, target, shift):
        copy = pltpu.make_async_remote_copy(
            src_ref=source,
            dst_ref=target,
            send_sem=self.send_sem.at[self.used],
            recv_sem=self.recv_sem.at[self.used],
            device_id=device_at(shift),
            device_id_type=MESH,
        )
        copy.start()
        self.used += 1
        self.started.append(copy)
        return copy


def lanczos_kernel(*refs, inputs, copies):
    hbm, (next_ref, corr_ref, norm_ref) = refs[:inputs], refs[inputs : inputs + 3]
    local = refs[inputs + 3 : 2 * inputs + 3]
    (idt, load_sem, send_sem, recv_sem, ext, work, mine, face, raw_land, low_land, up_land, back_raw, back_face,
     raw_back, low_back, up_back, stack, gram_tile, gram_land, row_tile, row_land, *hvp_scratch) = refs[2 * inputs + 3 :]
    places, basis, ids, counts, kinds, map_x, map_y, map_z, table, w1, w2, b1, b2, fo = local
    atoms = places.shape[2]
    stored = basis.shape[0]
    rows = stack.shape[0]
    pair = 2 * map_x.shape[1]
    sizes = sizes_of()
    entries = 3 * atoms * sizes[0] * sizes[1] * sizes[2]
    planes = plane_offsets()
    groups = reduction_groups()
    faces = ((1, low_land, up_back), (-1, up_land, low_back))

    partners = set()
    for dy, dz in planes:
        for dx in (-1, 0, 1):
            partners.add(tuple(step % peers for step, peers in zip((dx, dy, dz), sizes)))
    for _, _, shifts in groups:
        partners.update(shifts)
    partners = sorted(partners - {(0, 0, 0)})
    opposite = {tuple(-step % peers for step, peers in zip(shift, sizes)) for shift in partners}
    assert opposite == set(partners)
    barrier = pltpu.get_barrier_semaphore()
    for shift in partners:
        pl.semaphore_signal(barrier, inc=1, device_id=device_at(shift), device_id_type=MESH)
    loads = [pltpu.make_async_copy(a, b, load_sem.at[at]) for at, (a, b) in enumerate(zip(hbm, local))]
    for at in (0, 1, 5, 6, 7, 2, 3, 4, 8, 9, 10, 11, 12, 13):
        loads[at].start()
    early = lax.broadcasted_iota(jnp.int32, (8, pair), 1) < pair // 2
    line = lax.broadcasted_iota(jnp.int32, (8, pair), 0)
    for at in (0, 1, 5, 6, 7):
        loads[at].wait()
    for c in range(3):
        mine[c : c + 1, :] = places[c]
        mine[3 + c : 4 + c, :] = basis[stored - 1, c]
    map_rows = [jnp.concatenate([m[1:2, :], m[0:1, :]], axis=1).astype(F32) for m in (map_x, map_y, map_z)]
    mine[6:7, :] = map_rows[1]
    mine[7:8, :] = map_rows[2]
    pick_x = chosen_columns(map_rows[0], atoms)
    face[...] = select_dot(mine[...], pick_x, ((1,), (0,)))
    pl.semaphore_wait(barrier, len(partners))

    sender = Sender(send_sem, recv_sem)
    arriving = []
    for at, (dy, dz) in reversed(list(enumerate(planes))):
        for dx, land, _ in faces:
            arriving.append(sender.send(face, land.at[at], (dx, -dy, -dz)))
        if at:
            arriving.append(sender.send(mine, raw_land.at[at], (0, -dy, -dz)))

    stack[rows - 8 :, :] = jnp.zeros((8, 3 * atoms), F32)
    for k in range(stored):
        for c in range(3):
            stack[k : k + 1, c * atoms : (c + 1) * atoms] = basis[k, c]
    gram = dot_full(stack[...], stack[...], ((1,), (1,)))
    gram_tile[...] = jnp.concatenate([gram[r : r + 8] for r in range(0, rows, 8)], axis=1)
    for at in (2, 3, 4, 8, 9, 10, 11, 12, 13):
        loads[at].wait()
    idt[...] = ids[...].T
    for copy in arriving:
        copy.wait_recv()

    def shifted(x, row):
        return x + jnp.where(line == row, jnp.where(early, -1.0, 1.0), 0.0)

    raw = {plane: mine[...] if at == 0 else raw_land[at] for at, plane in enumerate(planes)}
    wide = {
        plane: jnp.concatenate([raw[plane], shifted(jnp.where(early, low_land[at], up_land[at]), 0)], axis=1)
        for at, plane in enumerate(planes)
    }
    pick_y, pick_z, wider = {}, {}, {}
    for dz in sorted({dz for _, dz in planes}):
        got = {}
        for dy in (1, -1):
            if (dy, dz) in raw:
                pick_y[dy, dz] = chosen_columns(raw[dy, dz][6:7, :], atoms + pair)
                got[dy] = select_dot(wide[dy, dz], pick_y[dy, dz], ((1,), (0,)))
        wider[dz] = jnp.concatenate([wide[0, dz], shifted(sides(got, early), 1)], axis=1)
    got = {}
    for dz in (1, -1):
        if dz in wider:
            pick_z[dz] = chosen_columns(raw[0, dz][7:8, :], atoms + 2 * pair)
            got[dz] = select_dot(wider[dz], pick_z[dz], ((1,), (0,)))
    ext[:, : atoms + 2 * pair] = wider[0]
    ext[:, atoms + 2 * pair :] = shifted(sides(got, early), 2)

    started = []
    members, _, shifts = groups[0]
    me = place_in(members)
    gram_land[me] = gram_tile[...]
    for shift in shifts:
        started.append(sender.send(gram_land.at[me], gram_land.at[me], shift))

    hessian_product(ext, idt, counts, kinds, table, w1, w2, b1, b2, fo, work, *hvp_scratch)

    many_y, many_z = -1 in {dy for dy, _ in planes}, -1 in wider
    back = {0: work[:, : atoms + 2 * pair]}
    for dz in pick_z:
        part = one_side(work[:, atoms + 2 * pair :], dz, many_z, early)
        back[dz] = select_dot(part, pick_z[dz], ((1,), (1,)))
    terms = {(0, dz): x[:, : atoms + pair] for dz, x in back.items()}
    for dy, dz in pick_y:
        part = one_side(back[dz][:, atoms + pair :], dy, many_y, early)
        terms[dy, dz] = select_dot(part, pick_y[dy, dz], ((1,), (1,)))
    arriving = []
    for at, (dy, dz) in reversed(list(enumerate(planes))):
        back_raw[at] = terms[dy, dz][:, :atoms]
        back_face[at] = terms[dy, dz][:, atoms:]
        for dx, _, land in faces:
            arriving.append(sender.send(back_face.at[at], land.at[at], (-dx, dy, dz)))
        if at:
            arriving.append(sender.send(back_raw.at[at], raw_back.at[at], (0, dy, dz)))

    for copy in started:
        copy.wait_recv()
    total = gram_land[0]
    for other in range(1, groups[0][1]):
        total = total + gram_land[other]
    base = groups[0][1]
    for members, count, shifts in groups[1:]:
        me = base + place_in(members)
        gram_land[me] = total
        started = [sender.send(gram_land.at[me], gram_land.at[me], shift) for shift in shifts]
        for copy in started:
            copy.wait_recv()
        total = gram_land[base]
        for other in range(1, count):
            total = total + gram_land[base + other]
        base += count
    gram = jnp.concatenate([total[:, r : r + rows] for r in range(0, rows * rows // 8, rows)], axis=0) / entries

    for copy in arriving:
        copy.wait_recv()
    own = back_raw[0]
    low, up = low_back[0], up_back[0]
    for at in range(1, len(planes)):
        own = own + raw_back[at]
        low = low + low_back[at]
        up = up + up_back[at]
    own = own + select_dot(jnp.where(early, up, low), pick_x, ((1,), (1,)))
    hv = jnp.concatenate([own[c : c + 1, :] for c in range(3)], axis=1)
    stack[stored : stored + 1, :] = hv
    sums = dot_full(jnp.broadcast_to(hv, (8, 3 * atoms)), stack[...], ((1,), (1,)))
    sums = jnp.concatenate([sums[0:1], jnp.zeros((1, row_tile.shape[1] - rows), F32)], axis=1)
    base = 0
    for members, count, shifts in groups:
        me = base + place_in(members)
        row_land[me] = sums
        started = [sender.send(row_land.at[me], row_land.at[me], shift) for shift in shifts]
        for copy in started:
            copy.wait_recv()
        sums = row_land[base]
        for other in range(1, count):
            sums = sums + row_land[base + other]
        base += count
    for copy in sender.started:
        copy.wait_send()
    assert sender.used == copies
    lane = lax.broadcasted_iota(jnp.int32, (1, rows), 1)
    sums = sums[:, :rows] / entries
    kept = jnp.where(lane < stored, sums, 0.0)
    both = jnp.concatenate([gram, stack[...]], axis=1)
    mixed = dot_full(jnp.broadcast_to(kept, (8, rows)), both, ((1,), (0,)))[0:1]
    plain = sums[:, stored : stored + 1]
    cross = jnp.sum(mixed[:, :rows] * kept - 2.0 * kept * kept, axis=1, keepdims=True)
    norm = jnp.sqrt(plain + cross + 1e-06)
    norm_ref[...] = norm
    corr_ref[...] = sums[:, :stored]
    for c in range(3):
        part = slice(c * atoms, (c + 1) * atoms)
        next_ref[c] = (hv[:, part] - mixed[:, rows:][:, part]) / norm


def on_device(positions, basis, neighbours, used_count, kinds, map_x, map_y, map_z,
              table, fit_w1, fit_b1, fit_w2, fit_b2, fit_out):
    atoms = positions.shape[-1]
    width = neighbours.shape[-1]
    stored = basis.shape[0]
    types, levels, m1 = table.shape
    m2 = fit_w1.shape[0] // m1
    pair = 2 * map_x.shape[-1]
    ext = atoms + 3 * pair
    args = [
        positions.reshape(3, 1, atoms),
        basis.reshape(stored, 3, 1, atoms),
        neighbours.reshape(atoms, width),
        used_count.reshape(1, atoms),
        kinds.reshape(1, atoms),
        map_x.reshape(2, -1),
        map_y.reshape(2, -1),
        map_z.reshape(2, -1),
        table,
        fit_w1.T,
        fit_w2,
        fit_b1[None],
        fit_b2[None],
        fit_out[None],
    ]
    rows = (stored + 8) // 8 * 8
    planes = len(plane_offsets())
    groups = reduction_groups()
    slots = sum(count for _, count, _ in groups)
    copies = 2 * (3 * planes - 1) + 2 * sum(len(shifts) for _, _, shifts in groups)
    any_space = pl.BlockSpec(memory_space=pl.ANY)
    vmem = pl.BlockSpec(memory_space=pltpu.VMEM)
    tile = pltpu.VMEM((planes, 8, pair), F32)
    next_vector, correlations, norm = pl.pallas_call(
        functools.partial(lanczos_kernel, inputs=len(args), copies=copies),
        out_shape=(
            jax.ShapeDtypeStruct((3, 1, atoms), F32),
            jax.ShapeDtypeStruct((1, stored), F32),
            jax.ShapeDtypeStruct((1, 1), F32),
        ),
        in_specs=[any_space] * len(args),
        out_specs=(vmem,) * 3,
        scratch_shapes=[pltpu.VMEM(x.shape, x.dtype) for x in args] + [
            pltpu.VMEM((width, atoms), jnp.int32),
            pltpu.SemaphoreType.DMA((len(args),)),
            pltpu.SemaphoreType.DMA((copies,)),
            pltpu.SemaphoreType.DMA((copies,)),
            pltpu.VMEM((8, ext), F32),
            pltpu.VMEM((8, ext), F32),
            pltpu.VMEM((8, pair), F32),
            pltpu.VMEM((8, pair), F32),
            tile, tile, tile, tile, tile, tile, tile, tile,
            pltpu.VMEM((rows, 3 * atoms), F32),
            pltpu.VMEM((8, rows * rows // 8), F32),
            pltpu.VMEM((slots, 8, rows * rows // 8), F32),
            pltpu.VMEM((1, 128), F32),
            pltpu.VMEM((slots, 1, 128), F32),
            pltpu.VMEM((6, width, atoms), F32),
            pltpu.VMEM((8, levels, 8, atoms), F32),
            pltpu.VMEM((8, m1, atoms), F32),
            pltpu.VMEM((m1 * m2, 2 * atoms), BF16),
            pltpu.VMEM((m1 * m2, 2 * atoms), BF16),
            pltpu.VMEM((m1 * m2, 2 * atoms), F32),
            pltpu.VMEM((8, m1, atoms), F32),
            pltpu.VMEM((8, levels, atoms), F32),
        ],
        compiler_params=pltpu.CompilerParams(
            collective_id=0, has_side_effects=True, vmem_limit_bytes=60 << 20
        ),
        name="lanczos",
    )(*args)
    return next_vector.reshape(positions.shape), correlations.reshape(stored), norm.reshape(())


def solution(mesh):
    placed = (
        P(None, "gx", "gy", "gz", None),
        P(None, None, "gx", "gy", "gz", None),
        P("gx", "gy", "gz", None, None),
        P("gx", "gy", "gz", None),
        P("gx", "gy", "gz", None),
        P("gx", "gy", "gz", None, None),
        P("gx", "gy", "gz", None, None),
        P("gx", "gy", "gz", None, None),
        P(),
        P(),
        P(),
        P(),
        P(),
        P(),
    )
    return jax.shard_map(
        on_device,
        mesh=mesh,
        in_specs=placed,
        out_specs=(P(None, "gx", "gy", "gz", None), P(), P()),
        check_vma=False,
    )
```

time: 56.9 us -> 46 us (0.81)
  Pallas kernels: 50.4 us -> 41 us
  local copies, waits for them, and re-layouts: 3.68 us -> 2.37 us
    pallas_call x3 -> x1, Pallas kernels: 50.4 us -> 41 us  [on_device(): pl.pallas_call(functools.partial(lanczos_kernel, inputs=len(args), copies...]
    unnamed x24 -> x2, local copies, waits for them, and re-layouts: 3.68 us -> 2.37 us
where the time goes in v1:
time: 46 us; the launch traced here: 45.8 us
  Pallas kernels  41 us (89%)
  between operations  2.41 us (5%)
  local copies, waits for them, and re-layouts  2.37 us (5%)
    pallas_call x1, Pallas kernels, on_device(): pl.pallas_call(functools.partial(lanczos_kernel, inputs=len(args), copies...  41 us
    unnamed x2, local copies, waits for them, and re-layouts  2.37 us

profile of v1, /device:TPU:0, one launch (start us, length us, event | category | flops | bytes accessed | tf_op | source)
XLA Modules:
  0.0 45.8 jit_solution(10459164605232895764)
XLA Ops:
  0.6 41.0 %lanczos.1 = (f32[3,1,128]{2,1,0:T(1,128)}, f32[1,30]{1,0:T(1,128)}, f32[1,1]{1,0:T(1,128)}) custom-call(f32[3,1,128]{2,1,0:T(1,128)} %bitcast.20, f32[30,3,1,128]{3,2,1,0:T(1,128)} %bitcast.19, s32[128,128]{1,0:T(8,128)} %bitcast.18, s32[1,128]{1,0:T(1,128)} %bitcast.28, s32[1,128]{1,0:T(1,128)} %bitcast.29, s32[2,64]{1,0:T(2,128)} %bitcast.22, ...), custom_call_target="tpu_custom_call" | custom-call | tf_op jit(solution)/shard_map/lanczos/pallas_call | solution.py:563
  41.7 1.2 %copy.21 = f32[3,1,1,1,128]{4,3,2,1,0:T(1,128)} copy(f32[3,1,1,1,128]{4,3,2,1,0:T(1,128)} %bitcast.21) | data formatting | bytes 3072
  42.9 1.1 %copy.22 = f32[30]{0:T(128)} copy(f32[30]{0:T(128)} %bitcast.30) | data formatting | bytes 240

commit v2 on v1

--- a/solution.py
+++ b/solution.py
@@ -9,6 +9,7 @@
 
 F32, BF16 = jnp.float32, jnp.bfloat16
 HIGHEST = lax.Precision.HIGHEST
+CHUNK = 8
 
 
 def split(x):
@@ -16,92 +17,214 @@
     return high, (x - high.astype(F32)).astype(BF16)
 
 
-def dot_parts(left, right, dims):
-    def one(a, b):
-        return lax.dot_general(a, b, (dims, ((), ())), preferred_element_type=F32)
-
-    return one(left[0], right[0]) + (one(left[0], right[1]) + one(left[1], right[0]))
+def left_parts(x):
+    high, low = split(x)
+    return jnp.concatenate([high, low, high], axis=1)
+
+
+def right_parts(x):
+    high, low = split(x)
+    return jnp.concatenate([high, high, low], axis=0)
+
+
+def matmul(a, b):
+    return lax.dot_general(a, b, (((1,), (0,)), ((), ())), preferred_element_type=F32)
 
 
 def dot_full(a, b, dims):
     return lax.dot_general(a, b, (dims, ((), ())), precision=HIGHEST, preferred_element_type=F32)
 
 
-def radial_parts(d, v, mask):
-    q = d[0] * d[0] + d[1] * d[1] + d[2] * d[2]
-    qd = 2.0 * (d[0] * v[0] + d[1] * v[1] + d[2] * v[2])
-    w = 1.0 / (q + 0.01)
-    decay = jnp.exp(-q) * mask
-    s = decay * jnp.sqrt(w)
-    u = decay * w
-    s_q = -s * (1.0 + 0.5 * w)
-    u_q = -u * (1.0 + w)
-    shrink = 1.0 / (1.0 + s)
-    t_s = shrink * shrink
-    t_q = t_s * s_q
-    return q, qd, w, s, u, s_q, u_q, shrink, t_s, t_q
-
-
-def hessian_product(ext_ref, idt, counts_ref, kinds_ref, table_ref, w1_ref, w2_ref, b1_ref, b2_ref, fo_ref, out_ref,
-                    dv, pool, env, dhi, dlo, gd, genv, gp):
-    width, atoms = idt.shape
+def padded(x, rows, columns):
+    if columns > x.shape[1]:
+        x = jnp.concatenate([x, jnp.zeros((x.shape[0], columns - x.shape[1]), x.dtype)], axis=1)
+    if rows > x.shape[0]:
+        x = jnp.concatenate([x, jnp.zeros((rows - x.shape[0], x.shape[1]), x.dtype)], axis=0)
+    return x
+
+
+def up_to(n, step):
+    return (n + step - 1) // step * step
+
+
+def hvp_shapes(atoms, width, types, levels, m1, m2, fit):
+    fit_wide, m1_wide = up_to(fit, 128), up_to(m1, 128)
+    return dict(
+        idt=((width, atoms), jnp.int32),
+        onehot=((width // CHUNK, 128, CHUNK * atoms), BF16),
+        w1_right=((2 * fit, m1 * m2), BF16),
+        w1_left=((m1 * m2, 3 * fit_wide), BF16),
+        w2_right=((fit, 3 * fit_wide), BF16),
+        w2_left=((fit, 3 * fit_wide), BF16),
+        columns=((fit, 8), F32),
+        table_up=((types * up_to(m1, 8), 3 * levels * CHUNK), BF16),
+        table_down=((types * levels, 3 * m1_wide), BF16),
+        dv=((6, width, atoms), F32),
+        radial=((5, width, atoms), F32),
+        mix=((9, width, atoms), F32),
+        gauss=((3, levels, width, atoms), F32),
+        pool=((levels * CHUNK, 8 * atoms), F32),
+        env=((8, up_to(m1, 8), atoms), F32),
+        dhi=((m1 * m2, 2 * atoms), BF16),
+        dlo=((m1 * m2, 2 * atoms), BF16),
+        gd=((m1 * m2, 2 * atoms), F32),
+        genv=((8, m1_wide, atoms), F32),
+        gp=((levels, 8 * atoms), F32),
+        forces=((width * 8, atoms), F32),
+    )
+
+
+def prepare_matrices(h, table_ref, w1_ref, w2_ref, b1_ref, b2_ref, fo_ref):
     types, levels, m1 = table_ref.shape
-    m2 = w1_ref.shape[1] // m1
-    ext = ext_ref.shape[1]
-    banks = ext // 128
+    width = h.idt.shape[0]
+    fit = w1_ref.shape[0]
+    fit_wide = h.w1_left.shape[1] // 3
+    m1_wide = h.table_down.shape[1] // 3
+    high, low = split(w1_ref[...])
+    h.w1_right[:fit, :] = high
+    h.w1_right[fit:, :] = low
+    h.w1_left[...] = left_parts(padded(w1_ref[...], fit_wide, 0).T)
+    w2 = padded(w2_ref[...], fit_wide, fit_wide)
+    h.w2_left[...] = left_parts(w2[:fit])
+    h.w2_right[...] = left_parts(w2.T[:fit])
+    lines = jnp.concatenate([b1_ref[...], b2_ref[...], fo_ref[...], jnp.zeros((5, fit), F32)], axis=0)
+    same = lax.broadcasted_iota(jnp.int32, (8, 8), 0) == lax.broadcasted_iota(jnp.int32, (8, 8), 1)
+    h.columns[...] = dot_full(lines, jnp.where(same, 1.0, 0.0).astype(F32), ((0,), (0,)))
+    m1_rows = h.table_up.shape[0] // types
+    level = lax.broadcasted_iota(jnp.int32, (levels, levels * CHUNK), 0)
+    slot = lax.broadcasted_iota(jnp.int32, (levels, levels * CHUNK), 1)
+    spread = jnp.where(jnp.right_shift(slot, CHUNK.bit_length() - 1) == level, 1.0 / width, 0.0).astype(F32)
+    for t in range(types):
+        up = padded(dot_full(table_ref[t], spread, ((0,), (0,))), m1_rows, 0)
+        h.table_up[t * m1_rows : (t + 1) * m1_rows, :] = left_parts(up)
+        h.table_down[t * levels : (t + 1) * levels, :] = left_parts(padded(table_ref[t] / width, 0, m1_wide))
+    tail = m1 // 8 * 8
+    h.genv[:, tail:, :] = jnp.zeros((8, m1_wide - tail, h.genv.shape[2]), F32)
+    h.forces[...] = jnp.zeros_like(h.forces)
+
+
+def prepare_scatter(h, ids_ref):
+    width, atoms = h.idt.shape
+    h.idt[...] = ids_ref[...].T
+    column = lax.broadcasted_iota(jnp.int32, (128, atoms), 0)
+
+    def one(c, carry):
+        lane = jnp.bitwise_and(h.idt[pl.ds(pl.multiple_of(c * CHUNK, CHUNK), CHUNK), :], 127)
+        for r in range(CHUNK):
+            hit = jnp.where(lane[r : r + 1, :] == column, 1.0, 0.0)
+            h.onehot[c, :, r * atoms : (r + 1) * atoms] = hit.astype(BF16)
+        return carry
+
+    lax.fori_loop(0, width // CHUNK, one, 0)
+
+
+def pair_terms(h, ext_ref, counts):
+    width, atoms = h.idt.shape
+    levels = h.gauss.shape[1]
+    banks = ext_ref.shape[1] // 128
     top = float(levels - 1)
-    pool[...] = jnp.zeros_like(pool)
-    counts = counts_ref[...]
-    kinds = kinds_ref[...]
-
-    def used(first, rows):
-        slot = lax.broadcasted_iota(jnp.int32, (rows, atoms), 0) + first
-        return jnp.where(slot < counts, 1.0, 0.0).astype(F32)
-
-    def forward(c, carry):
-        first = pl.multiple_of(c * 8, 8)
-        idx = idt[pl.ds(first, 8), :]
+
+    def one(c, carry):
+        first = pl.multiple_of(c * CHUNK, CHUNK)
+        here = pl.ds(first, CHUNK)
+        idx = h.idt[here, :]
         lane = jnp.bitwise_and(idx, 127)
         bank = jnp.right_shift(idx, 7)
         fields = []
         for f in range(6):
             got = None
             for b in range(banks):
-                row = jnp.broadcast_to(ext_ref[f : f + 1, b * 128 : (b + 1) * 128], (8, 128))
+                row = jnp.broadcast_to(ext_ref[f : f + 1, b * 128 : (b + 1) * 128], (CHUNK, 128))
                 part = jnp.take_along_axis(row, lane, axis=1, mode="promise_in_bounds")
                 got = part if got is None else jnp.where(bank == b, part, got)
             got = got - ext_ref[f : f + 1, :atoms]
-            dv[f, pl.ds(first, 8), :] = got
+            h.dv[f, here, :] = got
             fields.append(got)
         d, v = fields[:3], fields[3:]
-        _, qd, _, s, u, s_q, u_q, shrink, _, t_q = radial_parts(d, v, used(first, 8))
+        slot = lax.broadcasted_iota(jnp.int32, (CHUNK, atoms), 0) + first
+        q = d[0] * d[0] + d[1] * d[1] + d[2] * d[2]
+        qd = 2.0 * (d[0] * v[0] + d[1] * v[1] + d[2] * v[2])
+        w = 1.0 / (q + 0.01)
+        decay = jnp.where(slot < counts, jnp.exp(-q), 0.0)
+        s = decay * jnp.sqrt(w)
+        u = decay * w
+        s_q = -s * (1.0 + 0.5 * w)
+        u_q = -u * (1.0 + w)
+        shrink = 1.0 / (1.0 + s)
+        for at, value in enumerate((qd, w, s, u, shrink)):
+            h.radial[at, here, :] = value
+        step = s_q * qd
+        for at, value in enumerate(
+            [-2.0 * top * shrink * shrink * step]
+            + [s] + [u * e for e in d]
+            + [step] + [u_q * qd * d[e] + u * v[e] for e in range(3)]
+        ):
+            h.mix[at, here, :] = value
         scaled = s * shrink * top
-        r = [s] + [u * e for e in d]
-        dr = [s_q * qd] + [u_q * qd * d[e] + u * v[e] for e in range(3)]
-        slope = -2.0 * top * t_q * qd
-        tr = [slope * e for e in r]
         for k in range(levels):
             y = scaled - float(k)
             phi = jnp.exp(-(y * y))
             psi = y * phi
-            for a in range(4):
-                pool[a, k] += phi * r[a]
-                pool[4 + a, k] += phi * dr[a] + psi * tr[a]
+            h.gauss[0, k, here, :] = phi
+            h.gauss[1, k, here, :] = psi
+            h.gauss[2, k, here, :] = y * psi
         return carry
 
-    lax.fori_loop(0, width // 8, forward, 0)
-    pooled = jnp.concatenate([jnp.sum(pool[a], axis=1) for a in range(8)], axis=1) / width
-    kinds8 = jnp.concatenate([kinds] * 8, axis=1)
-    chosen = None
-    for t in range(types):
-        part = dot_full(table_ref[t], pooled, ((0,), (0,)))
-        chosen = part if t == 0 else jnp.where(kinds8 == t, part, chosen)
-    for a in range(8):
-        env[a] = chosen[:, a * atoms : (a + 1) * atoms]
-    lead = [env[a, :m2, :] for a in range(8)]
+    lax.fori_loop(0, width // CHUNK, one, 0, unroll=2)
+
+
+def pooled_terms(h):
+    width, atoms = h.idt.shape
+    levels = h.gauss.shape[1]
+    together = 4
+    zero = jnp.zeros((CHUNK, atoms), F32)
+    for k0 in range(0, levels, together):
+
+        def one(c, acc):
+            here = pl.ds(pl.multiple_of(c * CHUNK, CHUNK), CHUNK)
+            slope = h.mix[0, here, :]
+            r = [h.mix[1 + a, here, :] for a in range(4)]
+            dr = [h.mix[5 + a, here, :] for a in range(4)]
+            out = []
+            for k in range(together):
+                phi = h.gauss[0, k0 + k, here, :]
+                psi = h.gauss[1, k0 + k, here, :] * slope
+                out += [acc[8 * k + a] + phi * r[a] for a in range(4)]
+                out += [acc[8 * k + 4 + a] + (phi * dr[a] + psi * r[a]) for a in range(4)]
+            return tuple(out)
+
+        acc = lax.fori_loop(0, width // CHUNK, one, (zero,) * (8 * together), unroll=2)
+        for k in range(together):
+            for a in range(8):
+                h.pool[(k0 + k) * CHUNK : (k0 + k + 1) * CHUNK, a * atoms : (a + 1) * atoms] = acc[8 * k + a]
+
+
+def of_kind(kinds8, parts):
+    out = parts[0]
+    for t in range(1, len(parts)):
+        out = jnp.where(kinds8 == t, parts[t], out)
+    return out
+
+
+def environment(h, kinds8, types):
+    m1_rows = h.table_up.shape[0] // types
+    atoms = h.idt.shape[1]
+    for half in range(4):
+        at = slice(half * 2 * atoms, (half + 1) * 2 * atoms)
+        both = matmul(h.table_up[...], right_parts(h.pool[:, at]))
+        mine = of_kind(kinds8[:, at], [both[t * m1_rows : (t + 1) * m1_rows] for t in range(types)])
+        h.env[2 * half] = mine[:, :atoms]
+        h.env[2 * half + 1] = mine[:, atoms:]
+
+
+def fitting_net(h, m1, m2):
+    fit = h.columns.shape[0]
+    fit_wide = h.w2_left.shape[1] // 3
+    atoms = h.idt.shape[1]
+    lead = [h.env[a, :m2, :] for a in range(8)]
 
     def describe(m, carry):
-        rows = [env[a, pl.ds(m, 1), :] for a in range(8)]
+        rows = [h.env[a, pl.ds(m, 1), :] for a in range(8)]
         plain = rows[0] * lead[0]
         moved = rows[4] * lead[0] + rows[0] * lead[4]
         for a in range(1, 4):
@@ -110,90 +233,87 @@
         place = pl.ds(pl.multiple_of(m * m2, m2), m2)
         for at, value in ((0, plain), (1, moved)):
             high, low = split(value)
-            dhi[place, at * atoms : (at + 1) * atoms] = high
-            dlo[place, at * atoms : (at + 1) * atoms] = low
+            h.dhi[place, at * atoms : (at + 1) * atoms] = high
+            h.dlo[place, at * atoms : (at + 1) * atoms] = low
         return carry
 
     lax.fori_loop(0, m1, describe, 0, unroll=4)
-    w1 = split(w1_ref[...])
-    z1 = dot_parts(w1, (dhi[...], dlo[...]), ((1,), (0,)))
-    fit = b1_ref.shape[1]
-    lines = jnp.concatenate([b1_ref[...], b2_ref[...], fo_ref[...], jnp.zeros((5, fit), F32)], axis=0)
-    same = lax.broadcasted_iota(jnp.int32, (8, 8), 0) == lax.broadcasted_iota(jnp.int32, (8, 8), 1)
-    cols = dot_full(lines, jnp.where(same, 1.0, 0.0).astype(F32), ((0,), (0,)))
-    b1, b2, fo = cols[:, 0:1], cols[:, 1:2], cols[:, 2:3]
+    both = matmul(h.w1_right[...], h.dhi[...])
+    z1 = (both[:fit] + both[fit:]) + matmul(h.w1_right[:fit, :], h.dlo[...])
+    b1, b2, fo = h.columns[:, 0:1], h.columns[:, 1:2], h.columns[:, 2:3]
     h1 = jnp.tanh(z1[:, :atoms] + b1)
     gate1 = 1.0 - h1 * h1
     dh1 = gate1 * z1[:, atoms:]
-    w2 = w2_ref[...]
-    z2 = dot_full(w2, jnp.concatenate([h1, dh1], axis=1), ((0,), (0,)))
+    z2 = matmul(h.w2_right[...], right_parts(padded(jnp.concatenate([h1, dh1], axis=1), fit_wide, 0)))
     t2 = jnp.tanh(z2[:, :atoms] + b2)
     gate2 = 1.0 - t2 * t2
     dt2 = gate2 * z2[:, atoms:]
     gz2 = jnp.concatenate([fo * gate2, fo * (-2.0 * t2 * dt2)], axis=1)
-    gh = dot_full(w2, gz2, ((1,), (0,)))
+    gh = matmul(h.w2_left[...], right_parts(padded(gz2, fit_wide, 0)))
     gh1 = gh[:, :atoms] + fo
     gz1 = jnp.concatenate([gh1 * gate1, gh[:, atoms:] * gate1 - 2.0 * gh1 * h1 * dh1], axis=1)
-    gd[...] = dot_parts(w1, split(gz1), ((0,), (0,)))
+    h.gd[...] = matmul(h.w1_left[...], right_parts(padded(gz1, fit_wide, 0)))
 
     def describe_back(m, acc):
         place = pl.ds(pl.multiple_of(m * m2, m2), m2)
-        g = gd[place, :atoms]
-        dg = gd[place, atoms:]
-        out = []
+        g = h.gd[place, :atoms]
+        dg = h.gd[place, atoms:]
+        rows = [h.env[a, pl.ds(m, 1), :] for a in range(8)]
         for a in range(4):
-            genv[a, pl.ds(m, 1), :] = jnp.sum(g * lead[a], axis=0, keepdims=True)
-            genv[4 + a, pl.ds(m, 1), :] = jnp.sum(
+            h.genv[a, pl.ds(m, 1), :] = jnp.sum(g * lead[a], axis=0, keepdims=True)
+            h.genv[4 + a, pl.ds(m, 1), :] = jnp.sum(
                 dg * lead[a] + g * lead[4 + a], axis=0, keepdims=True
             )
-        for a in range(4):
-            out.append(acc[a] + g * env[a, pl.ds(m, 1), :])
-        for a in range(4):
-            out.append(
-                acc[4 + a]
-                + dg * env[a, pl.ds(m, 1), :]
-                + g * env[4 + a, pl.ds(m, 1), :]
-            )
+        out = [acc[a] + g * rows[a] for a in range(4)]
+        out += [acc[4 + a] + (dg * rows[a] + g * rows[4 + a]) for a in range(4)]
         return tuple(out)
 
     acc = lax.fori_loop(0, m1, describe_back, tuple(jnp.zeros((m2, atoms), F32) for _ in range(8)), unroll=2)
     for a in range(8):
-        genv[a, :m2, :] += acc[a]
-    total = None
-    pulled = jnp.concatenate([genv[a] for a in range(8)], axis=1)
-    for t in range(types):
-        part = dot_full(table_ref[t], jnp.where(kinds8 == t, pulled, 0.0), ((1,), (0,)))
-        total = part if total is None else total + part
-    total = total / width
-    for a in range(8):
-        gp[a] = total[:, a * atoms : (a + 1) * atoms]
-    low_iota = lax.broadcasted_iota(jnp.int32, (128, atoms), 0)
-
-    def backward(c, carry):
-        acc, centre = carry
-        first = pl.multiple_of(c * 8, 8)
-        d = [dv[f, pl.ds(first, 8), :] for f in range(3)]
-        v = [dv[f, pl.ds(first, 8), :] for f in range(3, 6)]
-        q, qd, w, s, u, s_q, u_q, shrink, t_s, t_q = radial_parts(d, v, used(first, 8))
+        h.genv[a, :m2, :] += acc[a]
+
+
+def pulled_back(h, kinds8, types):
+    levels = h.gp.shape[0]
+    atoms = h.idt.shape[1]
+    for half in range(4):
+        at = slice(half * 2 * atoms, (half + 1) * 2 * atoms)
+        pulled = jnp.concatenate([h.genv[2 * half], h.genv[2 * half + 1]], axis=1)
+        both = matmul(h.table_down[...], right_parts(pulled))
+        h.gp[:, at] = of_kind(kinds8[:, at], [both[t * levels : (t + 1) * levels] for t in range(types)])
+
+
+def pair_forces(h, out_ref):
+    width, atoms = h.idt.shape
+    levels = h.gauss.shape[1]
+    banks = out_ref.shape[1] // 128
+    top = float(levels - 1)
+
+    def force_of(c, centre):
+        first = pl.multiple_of(c * CHUNK, CHUNK)
+        here = pl.ds(first, CHUNK)
+        zero = jnp.zeros((CHUNK, atoms), F32)
+        s0, s1, s2, e0, e1 = ([zero] * 4 for _ in range(5))
+        for k in range(levels):
+            phi, psi, chi = (h.gauss[p, k, here, :] for p in range(3))
+            for a in range(4):
+                g = h.gp[k : k + 1, a * atoms : (a + 1) * atoms]
+                gd = h.gp[k : k + 1, (4 + a) * atoms : (5 + a) * atoms]
+                s0[a] = s0[a] + g * phi
+                s1[a] = s1[a] + g * psi
+                s2[a] = s2[a] + g * chi
+                e0[a] = e0[a] + gd * phi
+                e1[a] = e1[a] + gd * psi
+        d = [h.dv[f, here, :] for f in range(3)]
+        v = [h.dv[f, here, :] for f in range(3, 6)]
+        qd, w, s, u, shrink = (h.radial[at, here, :] for at in range(5))
+        s_q = -s * (1.0 + 0.5 * w)
+        u_q = -u * (1.0 + w)
+        t_s = shrink * shrink
+        t_q = t_s * s_q
         s_qq = -s_q * (1.0 + 0.5 * w) + 0.5 * s * w * w
         u_qq = -u_q * (1.0 + w) + u * w * w
         t_qq = -2.0 * t_s * shrink * s_q * s_q + t_s * s_qq
-        scaled = s * shrink * top
-        zero = jnp.zeros((8, atoms), F32)
-        s0, s1, s2, e0, e1 = ([zero] * 4 for _ in range(5))
-        for k in range(levels):
-            y = scaled - float(k)
-            phi = jnp.exp(-(y * y))
-            psi = y * phi
-            chi = y * psi
-            for a in range(4):
-                g = gp[a, k : k + 1, :]
-                h = gp[4 + a, k : k + 1, :]
-                s0[a] = s0[a] + g * phi
-                s1[a] = s1[a] + g * psi
-                s2[a] = s2[a] + g * chi
-                e0[a] = e0[a] + h * phi
-                e1[a] = e1[a] + h * psi
         step = t_q * qd
         val = s0
         val_t = [-2.0 * top * e for e in s1]
@@ -204,52 +324,61 @@
         big_t = val_t[1] * d[0] + val_t[2] * d[1] + val_t[3] * d[2]
         dbig = sum(dval[1 + e] * d[e] + val[1 + e] * v[e] for e in range(3))
         dbig_t = sum(dval_t[1 + e] * d[e] + val_t[1 + e] * v[e] for e in range(3))
-        kern = t_q * (val_t[0] * s + big_t * u) + val[0] * s_q + big * u_q
+        flow = val_t[0] * s + big_t * u
+        kern = t_q * flow + val[0] * s_q + big * u_q
         dkern = (
             t_q * (dval_t[0] * s + dbig_t * u)
             + dval[0] * s_q
             + dbig * u_q
-            + qd * (
-                t_qq * (val_t[0] * s + big_t * u)
-                + t_q * (val_t[0] * s_q + big_t * u_q)
-                + val[0] * s_qq
-                + big * u_qq
-            )
+            + qd * (t_qq * flow + t_q * (val_t[0] * s_q + big_t * u_q) + val[0] * s_qq + big * u_qq)
         )
         du = u_q * qd
-        force = [2.0 * (v[e] * kern + d[e] * dkern) + du * val[1 + e] + u * dval[1 + e] for e in range(3)]
-        centre = tuple(centre[e] - force[e] for e in range(3))
-        idx = idt[pl.ds(first, 8), :]
-        lane = jnp.bitwise_and(idx, 127)
-        bank = jnp.right_shift(idx, 7)
-        rows = []
+        out = []
         for e in range(3):
-            high = force[e].astype(BF16).astype(F32)
-            for part in (high, force[e] - high):
-                for b in range(banks):
-                    rows.append(jnp.where(bank == b, part, 0.0))
-        lefts, rights = [], []
-        for r in range(8):
-            lefts.append(jnp.concatenate([x[r : r + 1, :] for x in rows], axis=0).astype(BF16))
-            rights.append(jnp.where(lane[r : r + 1, :] == low_iota, 1.0, 0.0).astype(BF16))
-        acc = acc + lax.dot_general(
-            jnp.concatenate(lefts, axis=1),
-            jnp.concatenate(rights, axis=1),
-            (((1,), (1,)), ((), ())),
-            preferred_element_type=F32,
+            force = 2.0 * (v[e] * kern + d[e] * dkern) + du * val[1 + e] + u * dval[1 + e]
+            high = force.astype(BF16).astype(F32)
+            h.forces[pl.ds(first * 8 + e, CHUNK, stride=8), :] = high
+            h.forces[pl.ds(first * 8 + 3 + e, CHUNK, stride=8), :] = force - high
+            out.append(centre[e] - force)
+        return tuple(out)
+
+    zero = jnp.zeros((CHUNK, atoms), F32)
+    centre = lax.fori_loop(0, width // CHUNK, force_of, (zero,) * 3)
+
+    def scatter(c, acc):
+        first = pl.multiple_of(c * CHUNK, CHUNK)
+        bank = jnp.right_shift(h.idt[pl.ds(first, CHUNK), :], 7)
+        lefts = []
+        for r in range(CHUNK):
+            part = h.forces[pl.ds(pl.multiple_of((first + r) * 8, 8), 8), :]
+            mine = jnp.broadcast_to(bank[r : r + 1, :], part.shape)
+            lefts.append(jnp.concatenate([jnp.where(mine == b, part, 0.0) for b in range(banks)], axis=0).astype(BF16))
+        return acc + lax.dot_general(
+            jnp.concatenate(lefts, axis=1), h.onehot[c], (((1,), (1,)), ((), ())), preferred_element_type=F32
         )
-        return acc, centre
-
-    out_ref[...] = jnp.zeros_like(out_ref)
-    start = (jnp.zeros((6 * banks, 128), F32), tuple(jnp.zeros((8, atoms), F32) for _ in range(3)))
-    acc, centre = lax.fori_loop(0, width // 8, backward, start)
+
+    acc = lax.fori_loop(0, width // CHUNK, scatter, jnp.zeros((8 * banks, 128), F32))
+    for b in range(banks):
+        part = acc[8 * b : 8 * b + 8]
+        out_ref[:, b * 128 : (b + 1) * 128] = part + jnp.concatenate([part[3:], part[:3]], axis=0)
     for e in range(3):
-        base = 2 * banks * e
-        for b in range(banks):
-            row = acc[base + b : base + b + 1] + acc[base + banks + b : base + banks + b + 1]
-            if b == 0:
-                row = row + jnp.sum(centre[e], axis=0, keepdims=True)
-            out_ref[e : e + 1, b * 128 : (b + 1) * 128] = row
+        out_ref[e : e + 1, :atoms] += jnp.sum(centre[e], axis=0, keepdims=True)
+
+
+def hessian_product(h, ext_ref, counts_ref, kinds_ref, out_ref, types, m1, m2):
+    kinds8 = jnp.concatenate([kinds_ref[...]] * 8, axis=1)
+    pair_terms(h, ext_ref, counts_ref[...])
+    pooled_terms(h)
+    environment(h, kinds8, types)
+    fitting_net(h, m1, m2)
+    pulled_back(h, kinds8, types)
+    pair_forces(h, out_ref)
+
+
+class Scratch:
+    def __init__(self, names, refs):
+        for name, ref in zip(names, refs, strict=True):
+            setattr(self, name, ref)
 
 
 AXES = ("gx", "gy", "gz")
@@ -351,12 +480,15 @@
         return copy
 
 
-def lanczos_kernel(*refs, inputs, copies):
+def lanczos_kernel(*refs, inputs, copies, names):
     hbm, (next_ref, corr_ref, norm_ref) = refs[:inputs], refs[inputs : inputs + 3]
     local = refs[inputs + 3 : 2 * inputs + 3]
-    (idt, load_sem, send_sem, recv_sem, ext, work, mine, face, raw_land, low_land, up_land, back_raw, back_face,
+    (load_sem, send_sem, recv_sem, ext, work, mine, face, raw_land, low_land, up_land, back_raw, back_face,
      raw_back, low_back, up_back, stack, gram_tile, gram_land, row_tile, row_land, *hvp_scratch) = refs[2 * inputs + 3 :]
     places, basis, ids, counts, kinds, map_x, map_y, map_z, table, w1, w2, b1, b2, fo = local
+    h = Scratch(names, hvp_scratch)
+    types, _, m1 = table.shape
+    m2 = w1.shape[1] // m1
     atoms = places.shape[2]
     stored = basis.shape[0]
     rows = stack.shape[0]
@@ -412,7 +544,8 @@
     gram_tile[...] = jnp.concatenate([gram[r : r + 8] for r in range(0, rows, 8)], axis=1)
     for at in (2, 3, 4, 8, 9, 10, 11, 12, 13):
         loads[at].wait()
-    idt[...] = ids[...].T
+    prepare_scatter(h, ids)
+    prepare_matrices(h, table, w1, w2, b1, b2, fo)
     for copy in arriving:
         copy.wait_recv()
 
@@ -447,7 +580,7 @@
     for shift in shifts:
         started.append(sender.send(gram_land.at[me], gram_land.at[me], shift))
 
-    hessian_product(ext, idt, counts, kinds, table, w1, w2, b1, b2, fo, work, *hvp_scratch)
+    hessian_product(h, ext, counts, kinds, work, types, m1, m2)
 
     many_y, many_z = -1 in {dy for dy, _ in planes}, -1 in wider
     back = {0: work[:, : atoms + 2 * pair]}
@@ -557,11 +690,12 @@
     groups = reduction_groups()
     slots = sum(count for _, count, _ in groups)
     copies = 2 * (3 * planes - 1) + 2 * sum(len(shifts) for _, _, shifts in groups)
+    hvp = hvp_shapes(atoms, width, types, levels, m1, m2, fit_w2.shape[0])
     any_space = pl.BlockSpec(memory_space=pl.ANY)
     vmem = pl.BlockSpec(memory_space=pltpu.VMEM)
     tile = pltpu.VMEM((planes, 8, pair), F32)
     next_vector, correlations, norm = pl.pallas_call(
-        functools.partial(lanczos_kernel, inputs=len(args), copies=copies),
+        functools.partial(lanczos_kernel, inputs=len(args), copies=copies, names=tuple(hvp)),
         out_shape=(
             jax.ShapeDtypeStruct((3, 1, atoms), F32),
             jax.ShapeDtypeStruct((1, stored), F32),
@@ -570,7 +704,6 @@
         in_specs=[any_space] * len(args),
         out_specs=(vmem,) * 3,
         scratch_shapes=[pltpu.VMEM(x.shape, x.dtype) for x in args] + [
-            pltpu.VMEM((width, atoms), jnp.int32),
             pltpu.SemaphoreType.DMA((len(args),)),
             pltpu.SemaphoreType.DMA((copies,)),
             pltpu.SemaphoreType.DMA((copies,)),
@@ -584,15 +717,7 @@
             pltpu.VMEM((slots, 8, rows * rows // 8), F32),
             pltpu.VMEM((1, 128), F32),
             pltpu.VMEM((slots, 1, 128), F32),
-            pltpu.VMEM((6, width, atoms), F32),
-            pltpu.VMEM((8, levels, 8, atoms), F32),
-            pltpu.VMEM((8, m1, atoms), F32),
-            pltpu.VMEM((m1 * m2, 2 * atoms), BF16),
-            pltpu.VMEM((m1 * m2, 2 * atoms), BF16),
-            pltpu.VMEM((m1 * m2, 2 * atoms), F32),
-            pltpu.VMEM((8, m1, atoms), F32),
-            pltpu.VMEM((8, levels, atoms), F32),
-        ],
+        ] + [pltpu.VMEM(shape, dtype) for shape, dtype in hvp.values()],
         compiler_params=pltpu.CompilerParams(
             collective_id=0, has_side_effects=True, vmem_limit_bytes=60 << 20
         ),

time: 46 us -> 43.6 us (0.948)
  Pallas kernels: 41 us -> 38.6 us
    pallas_call x1, Pallas kernels: 41 us -> 38.6 us  [on_device(): pl.pallas_call(functools.partial(lanczos_kernel, inputs=len(args), copies...]
where the time goes in v2:
time: 43.6 us; the launch traced here: 43.4 us
  Pallas kernels  38.6 us (89%)
  between operations  2.41 us (6%)
  local copies, waits for them, and re-layouts  2.37 us (5%)
    pallas_call x1, Pallas kernels, on_device(): pl.pallas_call(functools.partial(lanczos_kernel, inputs=len(args), copies...  38.6 us
    unnamed x2, local copies, waits for them, and re-layouts  2.37 us

profile of v2, /device:TPU:0, one launch (start us, length us, event | category | flops | bytes accessed | tf_op | source)
XLA Modules:
  0.0 43.4 jit_solution(32635323579746913)
XLA Ops:
  0.6 38.6 %lanczos.1 = (f32[3,1,128]{2,1,0:T(1,128)}, f32[1,30]{1,0:T(1,128)}, f32[1,1]{1,0:T(1,128)}) custom-call(f32[3,1,128]{2,1,0:T(1,128)} %bitcast.20, f32[30,3,1,128]{3,2,1,0:T(1,128)} %bitcast.19, s32[128,128]{1,0:T(8,128)} %bitcast.18, s32[1,128]{1,0:T(1,128)} %bitcast.28, s32[1,128]{1,0:T(1,128)} %bitcast.29, s32[2,64]{1,0:T(2,128)} %bitcast.22, ...), custom_call_target="tpu_custom_call" | custom-call | tf_op jit(solution)/shard_map/lanczos/pallas_call | solution.py:697
  39.3 1.2 %copy.21 = f32[3,1,1,1,128]{4,3,2,1,0:T(1,128)} copy(f32[3,1,1,1,128]{4,3,2,1,0:T(1,128)} %bitcast.21) | data formatting | bytes 3072
  40.5 1.1 %copy.22 = f32[30]{0:T(128)} copy(f32[30]{0:T(128)} %bitcast.30) | data formatting | bytes 240

commit v3 on v2

--- a/solution.py
+++ b/solution.py
@@ -47,28 +47,29 @@
     return (n + step - 1) // step * step
 
 
-def hvp_shapes(atoms, width, types, levels, m1, m2, fit):
+def hvp_shapes(atoms, width, types, levels, m1, m2, fit, banks):
     fit_wide, m1_wide = up_to(fit, 128), up_to(m1, 128)
+    low = levels * m2
     return dict(
         idt=((width, atoms), jnp.int32),
-        onehot=((width // CHUNK, 128, CHUNK * atoms), BF16),
-        w1_right=((2 * fit, m1 * m2), BF16),
-        w1_left=((m1 * m2, 3 * fit_wide), BF16),
+        onehot=((width * atoms, 128), BF16),
+        in_bank=((banks, width, atoms), F32),
+        w1_rows=((fit_wide // 128, m1_wide * m2, 128), F32),
+        w1_low=((fit_wide // 128, types * low, 128), F32),
+        low_right=((types * fit, 3 * low), BF16),
+        low_left=((types * low, 3 * fit_wide), BF16),
         w2_right=((fit, 3 * fit_wide), BF16),
         w2_left=((fit, 3 * fit_wide), BF16),
         columns=((fit, 8), F32),
-        table_up=((types * up_to(m1, 8), 3 * levels * CHUNK), BF16),
-        table_down=((types * levels, 3 * m1_wide), BF16),
+        lead_up=((types * m2, 3 * levels), BF16),
+        lead_down=((types * levels, 3 * m2), BF16),
         dv=((6, width, atoms), F32),
         radial=((5, width, atoms), F32),
         mix=((9, width, atoms), F32),
         gauss=((3, levels, width, atoms), F32),
-        pool=((levels * CHUNK, 8 * atoms), F32),
-        env=((8, up_to(m1, 8), atoms), F32),
-        dhi=((m1 * m2, 2 * atoms), BF16),
-        dlo=((m1 * m2, 2 * atoms), BF16),
-        gd=((m1 * m2, 2 * atoms), F32),
-        genv=((8, m1_wide, atoms), F32),
+        pooled=((8, levels, atoms), F32),
+        product=((low, 2 * atoms), F32),
+        pulled=((low, 2 * atoms), F32),
         gp=((levels, 8 * atoms), F32),
         forces=((width * 8, atoms), F32),
     )
@@ -76,43 +77,56 @@
 
 def prepare_matrices(h, table_ref, w1_ref, w2_ref, b1_ref, b2_ref, fo_ref):
     types, levels, m1 = table_ref.shape
-    width = h.idt.shape[0]
-    fit = w1_ref.shape[0]
-    fit_wide = h.w1_left.shape[1] // 3
-    m1_wide = h.table_down.shape[1] // 3
-    high, low = split(w1_ref[...])
-    h.w1_right[:fit, :] = high
-    h.w1_right[fit:, :] = low
-    h.w1_left[...] = left_parts(padded(w1_ref[...], fit_wide, 0).T)
-    w2 = padded(w2_ref[...], fit_wide, fit_wide)
+    fit, m2 = w1_ref.shape[0], w1_ref.shape[1] // m1
+    halves, rows, _ = h.w1_rows.shape
+    m1_wide, low = rows // m2, levels * m2
+    turned = padded(w1_ref[...], halves * 128, 0).T
+    tables = jnp.concatenate([padded(table_ref[t], 0, m1_wide) for t in range(types)], axis=0)
+    tables = left_parts(tables)
+    for half in range(halves):
+        h.w1_rows[half, : m1 * m2, :] = turned[:, half * 128 : (half + 1) * 128]
+        h.w1_rows[half, m1 * m2 :, :] = jnp.zeros((rows - m1 * m2, 128), F32)
+    for n in range(m2):
+        part = [h.w1_rows[half, pl.ds(n, m1_wide, stride=m2), :] for half in range(halves)]
+        out = matmul(tables, right_parts(jnp.concatenate(part, axis=1)))
+        for half in range(halves):
+            h.w1_low[half, pl.ds(n, types * levels, stride=m2), :] = out[:, half * 128 : (half + 1) * 128]
+    for t in range(types):
+        at = slice(t * low, (t + 1) * low)
+        mine = jnp.concatenate([h.w1_low[half, at, :] for half in range(halves)], axis=1)
+        h.low_left[at, :] = left_parts(mine)
+        h.low_right[t * fit : (t + 1) * fit, :] = left_parts(mine.T[:fit])
+    w2 = padded(w2_ref[...], halves * 128, halves * 128)
     h.w2_left[...] = left_parts(w2[:fit])
     h.w2_right[...] = left_parts(w2.T[:fit])
     lines = jnp.concatenate([b1_ref[...], b2_ref[...], fo_ref[...], jnp.zeros((5, fit), F32)], axis=0)
-    same = lax.broadcasted_iota(jnp.int32, (8, 8), 0) == lax.broadcasted_iota(jnp.int32, (8, 8), 1)
-    h.columns[...] = dot_full(lines, jnp.where(same, 1.0, 0.0).astype(F32), ((0,), (0,)))
-    m1_rows = h.table_up.shape[0] // types
-    level = lax.broadcasted_iota(jnp.int32, (levels, levels * CHUNK), 0)
-    slot = lax.broadcasted_iota(jnp.int32, (levels, levels * CHUNK), 1)
-    spread = jnp.where(jnp.right_shift(slot, CHUNK.bit_length() - 1) == level, 1.0 / width, 0.0).astype(F32)
+    h.columns[...] = dot_full(lines, identity(8), ((0,), (0,)))
     for t in range(types):
-        up = padded(dot_full(table_ref[t], spread, ((0,), (0,))), m1_rows, 0)
-        h.table_up[t * m1_rows : (t + 1) * m1_rows, :] = left_parts(up)
-        h.table_down[t * levels : (t + 1) * levels, :] = left_parts(padded(table_ref[t] / width, 0, m1_wide))
-    tail = m1 // 8 * 8
-    h.genv[:, tail:, :] = jnp.zeros((8, m1_wide - tail, h.genv.shape[2]), F32)
+        first = table_ref[t][:, :m2]
+        h.lead_down[t * levels : (t + 1) * levels, :] = left_parts(first)
+        h.lead_up[t * m2 : (t + 1) * m2, :] = left_parts(dot_full(first, identity(levels), ((0,), (0,))))
     h.forces[...] = jnp.zeros_like(h.forces)
+
+
+def identity(n):
+    same = lax.broadcasted_iota(jnp.int32, (n, n), 0) == lax.broadcasted_iota(jnp.int32, (n, n), 1)
+    return jnp.where(same, 1.0, 0.0).astype(F32)
 
 
 def prepare_scatter(h, ids_ref):
     width, atoms = h.idt.shape
     h.idt[...] = ids_ref[...].T
-    column = lax.broadcasted_iota(jnp.int32, (128, atoms), 0)
+    bank = jnp.right_shift(h.idt[...], 7)
+    for b in range(h.in_bank.shape[0]):
+        h.in_bank[b] = jnp.where(bank == b, 1.0, 0.0).astype(F32)
+    lanes = lax.broadcasted_iota(jnp.int32, (atoms, 128), 1)
 
     def one(c, carry):
-        lane = jnp.bitwise_and(h.idt[pl.ds(pl.multiple_of(c * CHUNK, CHUNK), CHUNK), :], 127)
+        first = pl.multiple_of(c * CHUNK, CHUNK)
+        column = jnp.bitwise_and(h.idt[pl.ds(first, CHUNK), :], 127).T
         for r in range(CHUNK):
-            hit = jnp.where(lane[r : r + 1, :] == column, 1.0, 0.0)
-            h.onehot[c, :, r * atoms : (r + 1) * atoms] = hit.astype(BF16)
+            hit = jnp.where(column[:, r : r + 1] == lanes, 1.0, 0.0)
+            h.onehot[pl.ds(pl.multiple_of((first + r) * atoms, atoms), atoms), :] = hit.astype(BF16)
         return carry
 
     lax.fori_loop(0, width // CHUNK, one, 0)
@@ -196,50 +210,44 @@
         acc = lax.fori_loop(0, width // CHUNK, one, (zero,) * (8 * together), unroll=2)
         for k in range(together):
             for a in range(8):
-                h.pool[(k0 + k) * CHUNK : (k0 + k + 1) * CHUNK, a * atoms : (a + 1) * atoms] = acc[8 * k + a]
-
-
-def of_kind(kinds8, parts):
-    out = parts[0]
-    for t in range(1, len(parts)):
-        out = jnp.where(kinds8 == t, parts[t], out)
+                h.pooled[a, k0 + k : k0 + k + 1, :] = jnp.sum(acc[8 * k + a], axis=0, keepdims=True) / width
+
+
+def of_kind(kinds, rows):
+    types = len(kinds)
+    step = rows.shape[0] // types
+    out = rows[:step]
+    for t in range(1, types):
+        out = jnp.where(kinds[t], rows[t * step : (t + 1) * step], out)
     return out
 
 
-def environment(h, kinds8, types):
-    m1_rows = h.table_up.shape[0] // types
-    atoms = h.idt.shape[1]
-    for half in range(4):
-        at = slice(half * 2 * atoms, (half + 1) * 2 * atoms)
-        both = matmul(h.table_up[...], right_parts(h.pool[:, at]))
-        mine = of_kind(kinds8[:, at], [both[t * m1_rows : (t + 1) * m1_rows] for t in range(types)])
-        h.env[2 * half] = mine[:, :atoms]
-        h.env[2 * half + 1] = mine[:, atoms:]
-
-
-def fitting_net(h, m1, m2):
+def lanes_of(x, count, atoms):
+    return [x[:, a * atoms : (a + 1) * atoms] for a in range(count)]
+
+
+def fitting_net(h, kinds_ref, types):
     fit = h.columns.shape[0]
     fit_wide = h.w2_left.shape[1] // 3
-    atoms = h.idt.shape[1]
-    lead = [h.env[a, :m2, :] for a in range(8)]
-
-    def describe(m, carry):
-        rows = [h.env[a, pl.ds(m, 1), :] for a in range(8)]
+    levels = h.pooled.shape[1]
+    m2 = h.lead_up.shape[0] // types
+    width, atoms = h.idt.shape
+    kinds2 = jnp.concatenate([kinds_ref[...]] * 2, axis=1)
+    kinds8 = jnp.concatenate([kinds2] * 4, axis=1)
+    kinds2 = [kinds2 == t for t in range(types)]
+    kinds8 = [kinds8 == t for t in range(types)]
+    pooled = jnp.concatenate([h.pooled[a] for a in range(8)], axis=1)
+    lead = lanes_of(of_kind(kinds8, matmul(h.lead_up[...], right_parts(pooled))), 8, atoms)
+    for k in range(levels):
+        rows = [h.pooled[a, k : k + 1, :] for a in range(8)]
         plain = rows[0] * lead[0]
         moved = rows[4] * lead[0] + rows[0] * lead[4]
         for a in range(1, 4):
             plain += rows[a] * lead[a]
             moved += rows[4 + a] * lead[a] + rows[a] * lead[4 + a]
-        place = pl.ds(pl.multiple_of(m * m2, m2), m2)
-        for at, value in ((0, plain), (1, moved)):
-            high, low = split(value)
-            h.dhi[place, at * atoms : (at + 1) * atoms] = high
-            h.dlo[place, at * atoms : (at + 1) * atoms] = low
-        return carry
-
-    lax.fori_loop(0, m1, describe, 0, unroll=4)
-    both = matmul(h.w1_right[...], h.dhi[...])
-    z1 = (both[:fit] + both[fit:]) + matmul(h.w1_right[:fit, :], h.dlo[...])
+        h.product[k * m2 : (k + 1) * m2, :atoms] = plain
+        h.product[k * m2 : (k + 1) * m2, atoms:] = moved
+    z1 = of_kind(kinds2, matmul(h.low_right[...], right_parts(h.product[...])))
     b1, b2, fo = h.columns[:, 0:1], h.columns[:, 1:2], h.columns[:, 2:3]
     h1 = jnp.tanh(z1[:, :atoms] + b1)
     gate1 = 1.0 - h1 * h1
@@ -252,35 +260,21 @@
     gh = matmul(h.w2_left[...], right_parts(padded(gz2, fit_wide, 0)))
     gh1 = gh[:, :atoms] + fo
     gz1 = jnp.concatenate([gh1 * gate1, gh[:, atoms:] * gate1 - 2.0 * gh1 * h1 * dh1], axis=1)
-    h.gd[...] = matmul(h.w1_left[...], right_parts(padded(gz1, fit_wide, 0)))
-
-    def describe_back(m, acc):
-        place = pl.ds(pl.multiple_of(m * m2, m2), m2)
-        g = h.gd[place, :atoms]
-        dg = h.gd[place, atoms:]
-        rows = [h.env[a, pl.ds(m, 1), :] for a in range(8)]
+    h.pulled[...] = of_kind(kinds2, matmul(h.low_left[...], right_parts(padded(gz1, fit_wide, 0))))
+    acc = [jnp.zeros((m2, atoms), F32) for _ in range(8)]
+    for k in range(levels):
+        g = h.pulled[k * m2 : (k + 1) * m2, :atoms]
+        dg = h.pulled[k * m2 : (k + 1) * m2, atoms:]
+        rows = [h.pooled[a, k : k + 1, :] for a in range(8)]
         for a in range(4):
-            h.genv[a, pl.ds(m, 1), :] = jnp.sum(g * lead[a], axis=0, keepdims=True)
-            h.genv[4 + a, pl.ds(m, 1), :] = jnp.sum(
-                dg * lead[a] + g * lead[4 + a], axis=0, keepdims=True
-            )
-        out = [acc[a] + g * rows[a] for a in range(4)]
-        out += [acc[4 + a] + (dg * rows[a] + g * rows[4 + a]) for a in range(4)]
-        return tuple(out)
-
-    acc = lax.fori_loop(0, m1, describe_back, tuple(jnp.zeros((m2, atoms), F32) for _ in range(8)), unroll=2)
-    for a in range(8):
-        h.genv[a, :m2, :] += acc[a]
-
-
-def pulled_back(h, kinds8, types):
-    levels = h.gp.shape[0]
-    atoms = h.idt.shape[1]
-    for half in range(4):
-        at = slice(half * 2 * atoms, (half + 1) * 2 * atoms)
-        pulled = jnp.concatenate([h.genv[2 * half], h.genv[2 * half + 1]], axis=1)
-        both = matmul(h.table_down[...], right_parts(pulled))
-        h.gp[:, at] = of_kind(kinds8[:, at], [both[t * levels : (t + 1) * levels] for t in range(types)])
+            straight = jnp.sum(g * lead[a], axis=0, keepdims=True)
+            turned = jnp.sum(dg * lead[a] + g * lead[4 + a], axis=0, keepdims=True)
+            h.gp[k : k + 1, a * atoms : (a + 1) * atoms] = straight
+            h.gp[k : k + 1, (4 + a) * atoms : (5 + a) * atoms] = turned
+            acc[a] = acc[a] + g * rows[a]
+            acc[4 + a] = acc[4 + a] + (dg * rows[a] + g * rows[4 + a])
+    across = of_kind(kinds8, matmul(h.lead_down[...], right_parts(jnp.concatenate(acc, axis=1))))
+    h.gp[...] = (h.gp[...] + across) / width
 
 
 def pair_forces(h, out_ref):
@@ -345,19 +339,20 @@
     zero = jnp.zeros((CHUNK, atoms), F32)
     centre = lax.fori_loop(0, width // CHUNK, force_of, (zero,) * 3)
 
+    together = width // 2
+
     def scatter(c, acc):
-        first = pl.multiple_of(c * CHUNK, CHUNK)
-        bank = jnp.right_shift(h.idt[pl.ds(first, CHUNK), :], 7)
         lefts = []
-        for r in range(CHUNK):
-            part = h.forces[pl.ds(pl.multiple_of((first + r) * 8, 8), 8), :]
-            mine = jnp.broadcast_to(bank[r : r + 1, :], part.shape)
-            lefts.append(jnp.concatenate([jnp.where(mine == b, part, 0.0) for b in range(banks)], axis=0).astype(BF16))
-        return acc + lax.dot_general(
-            jnp.concatenate(lefts, axis=1), h.onehot[c], (((1,), (1,)), ((), ())), preferred_element_type=F32
-        )
-
-    acc = lax.fori_loop(0, width // CHUNK, scatter, jnp.zeros((8 * banks, 128), F32))
+        for r in range(together):
+            n = c * together + r
+            part = h.forces[pl.ds(pl.multiple_of(n * 8, 8), 8), :]
+            lefts.append(
+                jnp.concatenate([part * h.in_bank[b, pl.ds(n, 1), :] for b in range(banks)], axis=0).astype(BF16)
+            )
+        first = pl.multiple_of(c * together * atoms, together * atoms)
+        return acc + matmul(jnp.concatenate(lefts, axis=1), h.onehot[pl.ds(first, together * atoms), :])
+
+    acc = lax.fori_loop(0, width // together, scatter, jnp.zeros((8 * banks, 128), F32))
     for b in range(banks):
         part = acc[8 * b : 8 * b + 8]
         out_ref[:, b * 128 : (b + 1) * 128] = part + jnp.concatenate([part[3:], part[:3]], axis=0)
@@ -365,13 +360,10 @@
         out_ref[e : e + 1, :atoms] += jnp.sum(centre[e], axis=0, keepdims=True)
 
 
-def hessian_product(h, ext_ref, counts_ref, kinds_ref, out_ref, types, m1, m2):
-    kinds8 = jnp.concatenate([kinds_ref[...]] * 8, axis=1)
+def hessian_product(h, ext_ref, counts_ref, kinds_ref, out_ref, types):
     pair_terms(h, ext_ref, counts_ref[...])
     pooled_terms(h)
-    environment(h, kinds8, types)
-    fitting_net(h, m1, m2)
-    pulled_back(h, kinds8, types)
+    fitting_net(h, kinds_ref, types)
     pair_forces(h, out_ref)
 
 
@@ -487,8 +479,7 @@
      raw_back, low_back, up_back, stack, gram_tile, gram_land, row_tile, row_land, *hvp_scratch) = refs[2 * inputs + 3 :]
     places, basis, ids, counts, kinds, map_x, map_y, map_z, table, w1, w2, b1, b2, fo = local
     h = Scratch(names, hvp_scratch)
-    types, _, m1 = table.shape
-    m2 = w1.shape[1] // m1
+    types = table.shape[0]
     atoms = places.shape[2]
     stored = basis.shape[0]
     rows = stack.shape[0]
@@ -580,7 +571,7 @@
     for shift in shifts:
         started.append(sender.send(gram_land.at[me], gram_land.at[me], shift))
 
-    hessian_product(h, ext, counts, kinds, work, types, m1, m2)
+    hessian_product(h, ext, counts, kinds, work, types)
 
     many_y, many_z = -1 in {dy for dy, _ in planes}, -1 in wider
     back = {0: work[:, : atoms + 2 * pair]}
@@ -690,7 +681,7 @@
     groups = reduction_groups()
     slots = sum(count for _, count, _ in groups)
     copies = 2 * (3 * planes - 1) + 2 * sum(len(shifts) for _, _, shifts in groups)
-    hvp = hvp_shapes(atoms, width, types, levels, m1, m2, fit_w2.shape[0])
+    hvp = hvp_shapes(atoms, width, types, levels, m1, m2, fit_w2.shape[0], ext // 128)
     any_space = pl.BlockSpec(memory_space=pl.ANY)
     vmem = pl.BlockSpec(memory_space=pltpu.VMEM)
     tile = pltpu.VMEM((planes, 8, pair), F32)

time: 43.6 us -> 40.6 us (0.931)
  Pallas kernels: 38.6 us -> 35.6 us
    pallas_call x1, Pallas kernels: 38.6 us -> 35.6 us  [on_device(): pl.pallas_call(functools.partial(lanczos_kernel, inputs=len(args), copies...]
where the time goes in v3:
time: 40.6 us; the launch traced here: 40.4 us
  Pallas kernels  35.6 us (88%)
  between operations  2.41 us (6%)
  local copies, waits for them, and re-layouts  2.37 us (6%)
    pallas_call x1, Pallas kernels, on_device(): pl.pallas_call(functools.partial(lanczos_kernel, inputs=len(args), copies...  35.6 us
    unnamed x2, local copies, waits for them, and re-layouts  2.37 us

profile of v3, /device:TPU:0, one launch (start us, length us, event | category | flops | bytes accessed | tf_op | source)
XLA Modules:
  0.0 40.4 jit_solution(9940016091451935864)
XLA Ops:
  0.6 35.6 %lanczos.1 = (f32[3,1,128]{2,1,0:T(1,128)}, f32[1,30]{1,0:T(1,128)}, f32[1,1]{1,0:T(1,128)}) custom-call(f32[3,1,128]{2,1,0:T(1,128)} %bitcast.20, f32[30,3,1,128]{3,2,1,0:T(1,128)} %bitcast.19, s32[128,128]{1,0:T(8,128)} %bitcast.18, s32[1,128]{1,0:T(1,128)} %bitcast.28, s32[1,128]{1,0:T(1,128)} %bitcast.29, s32[2,64]{1,0:T(2,128)} %bitcast.22, ...), custom_call_target="tpu_custom_call" | custom-call | tf_op jit(solution)/shard_map/lanczos/pallas_call | solution.py:688
  36.3 1.2 %copy.21 = f32[3,1,1,1,128]{4,3,2,1,0:T(1,128)} copy(f32[3,1,1,1,128]{4,3,2,1,0:T(1,128)} %bitcast.21) | data formatting | bytes 3072
  37.5 1.1 %copy.22 = f32[30]{0:T(128)} copy(f32[30]{0:T(128)} %bitcast.30) | data formatting | bytes 240

commit v4 on v3

--- a/solution.py
+++ b/solution.py
@@ -10,6 +10,7 @@
 F32, BF16 = jnp.float32, jnp.bfloat16
 HIGHEST = lax.Precision.HIGHEST
 CHUNK = 8
+DIGIT = 64
 
 
 def split(x):
@@ -47,13 +48,13 @@
     return (n + step - 1) // step * step
 
 
-def hvp_shapes(atoms, width, types, levels, m1, m2, fit, banks):
+def hvp_shapes(atoms, width, types, levels, m1, m2, fit, ext):
     fit_wide, m1_wide = up_to(fit, 128), up_to(m1, 128)
     low = levels * m2
     return dict(
         idt=((width, atoms), jnp.int32),
-        onehot=((width * atoms, 128), BF16),
-        in_bank=((banks, width, atoms), F32),
+        onehot=((width // CHUNK, DIGIT, CHUNK * atoms), BF16),
+        in_bank=((ext // DIGIT, width, atoms), F32),
         w1_rows=((fit_wide // 128, m1_wide * m2, 128), F32),
         w1_low=((fit_wide // 128, types * low, 128), F32),
         low_right=((types * fit, 3 * low), BF16),
@@ -116,17 +117,16 @@
 def prepare_scatter(h, ids_ref):
     width, atoms = h.idt.shape
     h.idt[...] = ids_ref[...].T
-    bank = jnp.right_shift(h.idt[...], 7)
+    bank = jnp.right_shift(h.idt[...], DIGIT.bit_length() - 1)
     for b in range(h.in_bank.shape[0]):
         h.in_bank[b] = jnp.where(bank == b, 1.0, 0.0).astype(F32)
-    lanes = lax.broadcasted_iota(jnp.int32, (atoms, 128), 1)
+    column = lax.broadcasted_iota(jnp.int32, (DIGIT, atoms), 0)
 
     def one(c, carry):
-        first = pl.multiple_of(c * CHUNK, CHUNK)
-        column = jnp.bitwise_and(h.idt[pl.ds(first, CHUNK), :], 127).T
+        digit = jnp.bitwise_and(h.idt[pl.ds(pl.multiple_of(c * CHUNK, CHUNK), CHUNK), :], DIGIT - 1)
         for r in range(CHUNK):
-            hit = jnp.where(column[:, r : r + 1] == lanes, 1.0, 0.0)
-            h.onehot[pl.ds(pl.multiple_of((first + r) * atoms, atoms), atoms), :] = hit.astype(BF16)
+            hit = jnp.where(digit[r : r + 1, :] == column, 1.0, 0.0)
+            h.onehot[c, :, r * atoms : (r + 1) * atoms] = hit.astype(BF16)
         return carry
 
     lax.fori_loop(0, width // CHUNK, one, 0)
@@ -280,7 +280,7 @@
 def pair_forces(h, out_ref):
     width, atoms = h.idt.shape
     levels = h.gauss.shape[1]
-    banks = out_ref.shape[1] // 128
+    banks = h.in_bank.shape[0]
     top = float(levels - 1)
 
     def force_of(c, centre):
@@ -349,13 +349,16 @@
             lefts.append(
                 jnp.concatenate([part * h.in_bank[b, pl.ds(n, 1), :] for b in range(banks)], axis=0).astype(BF16)
             )
-        first = pl.multiple_of(c * together * atoms, together * atoms)
-        return acc + matmul(jnp.concatenate(lefts, axis=1), h.onehot[pl.ds(first, together * atoms), :])
-
-    acc = lax.fori_loop(0, width // together, scatter, jnp.zeros((8 * banks, 128), F32))
-    for b in range(banks):
-        part = acc[8 * b : 8 * b + 8]
-        out_ref[:, b * 128 : (b + 1) * 128] = part + jnp.concatenate([part[3:], part[:3]], axis=0)
+        right = jnp.concatenate([h.onehot[c * (together // CHUNK) + j] for j in range(together // CHUNK)], axis=1)
+        return acc + lax.dot_general(
+            jnp.concatenate(lefts, axis=1), right, (((1,), (1,)), ((), ())), preferred_element_type=F32
+        )
+
+    acc = lax.fori_loop(0, width // together, scatter, jnp.zeros((8 * banks, DIGIT), F32))
+    per = 128 // DIGIT
+    for b in range(0, banks, per):
+        part = jnp.concatenate([acc[8 * j : 8 * j + 8] for j in range(b, b + per)], axis=1)
+        out_ref[:, b * DIGIT : (b + per) * DIGIT] = part + jnp.concatenate([part[3:], part[:3]], axis=0)
     for e in range(3):
         out_ref[e : e + 1, :atoms] += jnp.sum(centre[e], axis=0, keepdims=True)
 
@@ -681,7 +684,7 @@
     groups = reduction_groups()
     slots = sum(count for _, count, _ in groups)
     copies = 2 * (3 * planes - 1) + 2 * sum(len(shifts) for _, _, shifts in groups)
-    hvp = hvp_shapes(atoms, width, types, levels, m1, m2, fit_w2.shape[0], ext // 128)
+    hvp = hvp_shapes(atoms, width, types, levels, m1, m2, fit_w2.shape[0], ext)
     any_space = pl.BlockSpec(memory_space=pl.ANY)
     vmem = pl.BlockSpec(memory_space=pltpu.VMEM)
     tile = pltpu.VMEM((planes, 8, pair), F32)

time: 40.6 us -> 35.9 us (0.88)
  Pallas kernels: 35.6 us -> 30.9 us
    pallas_call x1, Pallas kernels: 35.6 us -> 30.9 us  [on_device(): pl.pallas_call(functools.partial(lanczos_kernel, inputs=len(args), copies...]
where the time goes in v4:
time: 35.9 us; the launch traced here: 35.7 us
  Pallas kernels  30.9 us (86%)
  between operations  2.41 us (7%)
  local copies, waits for them, and re-layouts  2.37 us (7%)
    pallas_call x1, Pallas kernels, on_device(): pl.pallas_call(functools.partial(lanczos_kernel, inputs=len(args), copies...  30.9 us
    unnamed x2, local copies, waits for them, and re-layouts  2.37 us

profile of v4, /device:TPU:0, one launch (start us, length us, event | category | flops | bytes accessed | tf_op | source)
XLA Modules:
  0.0 35.7 jit_solution(6052763348773100507)
XLA Ops:
  0.6 30.9 %lanczos.1 = (f32[3,1,128]{2,1,0:T(1,128)}, f32[1,30]{1,0:T(1,128)}, f32[1,1]{1,0:T(1,128)}) custom-call(f32[3,1,128]{2,1,0:T(1,128)} %bitcast.20, f32[30,3,1,128]{3,2,1,0:T(1,128)} %bitcast.19, s32[128,128]{1,0:T(8,128)} %bitcast.18, s32[1,128]{1,0:T(1,128)} %bitcast.28, s32[1,128]{1,0:T(1,128)} %bitcast.29, s32[2,64]{1,0:T(2,128)} %bitcast.22, ...), custom_call_target="tpu_custom_call" | custom-call | tf_op jit(solution)/shard_map/lanczos/pallas_call | solution.py:691
  31.6 1.2 %copy.21 = f32[3,1,1,1,128]{4,3,2,1,0:T(1,128)} copy(f32[3,1,1,1,128]{4,3,2,1,0:T(1,128)} %bitcast.21) | data formatting | bytes 3072
  32.8 1.1 %copy.22 = f32[30]{0:T(128)} copy(f32[30]{0:T(128)} %bitcast.30) | data formatting | bytes 240

commit v5 on v4

--- a/solution.py
+++ b/solution.py
@@ -64,10 +64,10 @@
         columns=((fit, 8), F32),
         lead_up=((types * m2, 3 * levels), BF16),
         lead_down=((types * levels, 3 * m2), BF16),
-        dv=((6, width, atoms), F32),
-        radial=((5, width, atoms), F32),
-        mix=((9, width, atoms), F32),
-        gauss=((3, levels, width, atoms), F32),
+        dv=((6, width + CHUNK, atoms), F32),
+        radial=((5, width + CHUNK, atoms), F32),
+        mix=((9, width + CHUNK, atoms), F32),
+        gauss=((levels, 3, width + CHUNK, atoms), F32),
         pooled=((8, levels, atoms), F32),
         product=((low, 2 * atoms), F32),
         pulled=((low, 2 * atoms), F32),
@@ -134,7 +134,7 @@
 
 def pair_terms(h, ext_ref, counts):
     width, atoms = h.idt.shape
-    levels = h.gauss.shape[1]
+    levels = h.gauss.shape[0]
     banks = ext_ref.shape[1] // 128
     top = float(levels - 1)
 
@@ -179,35 +179,37 @@
             y = scaled - float(k)
             phi = jnp.exp(-(y * y))
             psi = y * phi
-            h.gauss[0, k, here, :] = phi
-            h.gauss[1, k, here, :] = psi
-            h.gauss[2, k, here, :] = y * psi
+            h.gauss[k, 0, here, :] = phi
+            h.gauss[k, 1, here, :] = psi
+            h.gauss[k, 2, here, :] = y * psi
         return carry
 
-    lax.fori_loop(0, width // CHUNK, one, 0, unroll=2)
+    lax.fori_loop(0, width // CHUNK, one, 0, unroll=8)
 
 
 def pooled_terms(h):
     width, atoms = h.idt.shape
-    levels = h.gauss.shape[1]
+    levels = h.gauss.shape[0]
     together = 4
     zero = jnp.zeros((CHUNK, atoms), F32)
     for k0 in range(0, levels, together):
 
         def one(c, acc):
-            here = pl.ds(pl.multiple_of(c * CHUNK, CHUNK), CHUNK)
+            here = slice(c * CHUNK, (c + 1) * CHUNK)
             slope = h.mix[0, here, :]
             r = [h.mix[1 + a, here, :] for a in range(4)]
             dr = [h.mix[5 + a, here, :] for a in range(4)]
             out = []
             for k in range(together):
-                phi = h.gauss[0, k0 + k, here, :]
-                psi = h.gauss[1, k0 + k, here, :] * slope
+                phi = h.gauss[k0 + k, 0, here, :]
+                psi = h.gauss[k0 + k, 1, here, :] * slope
                 out += [acc[8 * k + a] + phi * r[a] for a in range(4)]
                 out += [acc[8 * k + 4 + a] + (phi * dr[a] + psi * r[a]) for a in range(4)]
             return tuple(out)
 
-        acc = lax.fori_loop(0, width // CHUNK, one, (zero,) * (8 * together), unroll=2)
+        acc = (zero,) * (8 * together)
+        for c in range(width // CHUNK):
+            acc = one(c, acc)
         for k in range(together):
             for a in range(8):
                 h.pooled[a, k0 + k : k0 + k + 1, :] = jnp.sum(acc[8 * k + a], axis=0, keepdims=True) / width
@@ -279,7 +281,7 @@
 
 def pair_forces(h, out_ref):
     width, atoms = h.idt.shape
-    levels = h.gauss.shape[1]
+    levels = h.gauss.shape[0]
     banks = h.in_bank.shape[0]
     top = float(levels - 1)
 
@@ -289,7 +291,7 @@
         zero = jnp.zeros((CHUNK, atoms), F32)
         s0, s1, s2, e0, e1 = ([zero] * 4 for _ in range(5))
         for k in range(levels):
-            phi, psi, chi = (h.gauss[p, k, here, :] for p in range(3))
+            phi, psi, chi = (h.gauss[k, p, here, :] for p in range(3))
             for a in range(4):
                 g = h.gp[k : k + 1, a * atoms : (a + 1) * atoms]
                 gd = h.gp[k : k + 1, (4 + a) * atoms : (5 + a) * atoms]
@@ -456,30 +458,32 @@
     return jnp.where(early, x, 0.0) if step == -1 else jnp.where(early, 0.0, x)
 
 
-class Sender:
-    def __init__(self, send_sem, recv_sem):
-        self.send_sem, self.recv_sem, self.used, self.started = send_sem, recv_sem, 0, []
-
-    def send(self, source, target, shift):
-        copy = pltpu.make_async_remote_copy(
+class Round:
+    def __init__(self, sems, at, landed):
+        self.sems, self.at, self.landed = sems, at, landed
+
+    def copy(self, source, target, shift):
+        return pltpu.make_async_remote_copy(
             src_ref=source,
             dst_ref=target,
-            send_sem=self.send_sem.at[self.used],
-            recv_sem=self.recv_sem.at[self.used],
+            send_sem=self.sems.at[self.at, 0],
+            recv_sem=self.sems.at[self.at, 1],
             device_id=device_at(shift),
             device_id_type=MESH,
         )
-        copy.start()
-        self.used += 1
-        self.started.append(copy)
-        return copy
-
-
-def lanczos_kernel(*refs, inputs, copies, names):
+
+    def send(self, source, target, shift):
+        self.shift = shift
+        self.copy(source, target, shift).start()
+
+    def all_of_them(self):
+        return self.copy(self.landed, self.landed, self.shift)
+
+
+def lanczos_kernel(*refs, inputs, names):
     hbm, (next_ref, corr_ref, norm_ref) = refs[:inputs], refs[inputs : inputs + 3]
     local = refs[inputs + 3 : 2 * inputs + 3]
-    (load_sem, send_sem, recv_sem, ext, work, mine, face, raw_land, low_land, up_land, back_raw, back_face,
-     raw_back, low_back, up_back, stack, gram_tile, gram_land, row_tile, row_land, *hvp_scratch) = refs[2 * inputs + 3 :]
+    (load_sem, round_sem, ext, work, mine, face, landed, back_raw, back_face, returned, stack, gram_land, row_land, *hvp_scratch) = refs[2 * inputs + 3 :]
     places, basis, ids, counts, kinds, map_x, map_y, map_z, table, w1, w2, b1, b2, fo = local
     h = Scratch(names, hvp_scratch)
     types = table.shape[0]
@@ -491,7 +495,7 @@
     entries = 3 * atoms * sizes[0] * sizes[1] * sizes[2]
     planes = plane_offsets()
     groups = reduction_groups()
-    faces = ((1, low_land, up_back), (-1, up_land, low_back))
+    count = len(planes)
 
     partners = set()
     for dy, dz in planes:
@@ -522,33 +526,31 @@
     face[...] = select_dot(mine[...], pick_x, ((1,), (0,)))
     pl.semaphore_wait(barrier, len(partners))
 
-    sender = Sender(send_sem, recv_sem)
-    arriving = []
+    halo = Round(round_sem, 0, landed)
     for at, (dy, dz) in reversed(list(enumerate(planes))):
-        for dx, land, _ in faces:
-            arriving.append(sender.send(face, land.at[at], (dx, -dy, -dz)))
+        halo.send(face, landed.at[at], (1, -dy, -dz))
+        halo.send(face, landed.at[count + at], (-1, -dy, -dz))
         if at:
-            arriving.append(sender.send(mine, raw_land.at[at], (0, -dy, -dz)))
+            halo.send(mine, landed.at[2 * count + at - 1], (0, -dy, -dz))
 
     stack[rows - 8 :, :] = jnp.zeros((8, 3 * atoms), F32)
     for k in range(stored):
         for c in range(3):
             stack[k : k + 1, c * atoms : (c + 1) * atoms] = basis[k, c]
     gram = dot_full(stack[...], stack[...], ((1,), (1,)))
-    gram_tile[...] = jnp.concatenate([gram[r : r + 8] for r in range(0, rows, 8)], axis=1)
+    gram = jnp.concatenate([gram[r : r + 8] for r in range(0, rows, 8)], axis=1)
     for at in (2, 3, 4, 8, 9, 10, 11, 12, 13):
         loads[at].wait()
     prepare_scatter(h, ids)
     prepare_matrices(h, table, w1, w2, b1, b2, fo)
-    for copy in arriving:
-        copy.wait_recv()
+    halo.all_of_them().wait_recv()
 
     def shifted(x, row):
         return x + jnp.where(line == row, jnp.where(early, -1.0, 1.0), 0.0)
 
-    raw = {plane: mine[...] if at == 0 else raw_land[at] for at, plane in enumerate(planes)}
+    raw = {plane: mine[...] if at == 0 else landed[2 * count + at - 1] for at, plane in enumerate(planes)}
     wide = {
-        plane: jnp.concatenate([raw[plane], shifted(jnp.where(early, low_land[at], up_land[at]), 0)], axis=1)
+        plane: jnp.concatenate([raw[plane], shifted(jnp.where(early, landed[at], landed[count + at]), 0)], axis=1)
         for at, plane in enumerate(planes)
     }
     pick_y, pick_z, wider = {}, {}, {}
@@ -567,12 +569,22 @@
     ext[:, : atoms + 2 * pair] = wider[0]
     ext[:, atoms + 2 * pair :] = shifted(sides(got, early), 2)
 
-    started = []
-    members, _, shifts = groups[0]
-    me = place_in(members)
-    gram_land[me] = gram_tile[...]
-    for shift in shifts:
-        started.append(sender.send(gram_land.at[me], gram_land.at[me], shift))
+    def gather_from(group, kind, tiles, base, value):
+        members, size, shifts = groups[group]
+        me = base + place_in(members)
+        tiles[me] = value
+        around = Round(round_sem, 2 + 2 * group + kind, tiles.at[pl.ds(base, size - 1)])
+        for shift in shifts:
+            around.send(tiles.at[me], tiles.at[me], shift)
+        return around
+
+    def added(tiles, base, size):
+        total = tiles[base]
+        for other in range(1, size):
+            total = total + tiles[base + other]
+        return total
+
+    rounds = [halo, gather_from(0, 0, gram_land, 0, gram)]
 
     hessian_product(h, ext, counts, kinds, work, types)
 
@@ -585,60 +597,45 @@
     for dy, dz in pick_y:
         part = one_side(back[dz][:, atoms + pair :], dy, many_y, early)
         terms[dy, dz] = select_dot(part, pick_y[dy, dz], ((1,), (1,)))
-    arriving = []
+    back_round = Round(round_sem, 1, returned)
     for at, (dy, dz) in reversed(list(enumerate(planes))):
         back_raw[at] = terms[dy, dz][:, :atoms]
         back_face[at] = terms[dy, dz][:, atoms:]
-        for dx, _, land in faces:
-            arriving.append(sender.send(back_face.at[at], land.at[at], (-dx, dy, dz)))
+        back_round.send(back_face.at[at], returned.at[at], (-1, dy, dz))
+        back_round.send(back_face.at[at], returned.at[count + at], (1, dy, dz))
         if at:
-            arriving.append(sender.send(back_raw.at[at], raw_back.at[at], (0, dy, dz)))
-
-    for copy in started:
-        copy.wait_recv()
-    total = gram_land[0]
-    for other in range(1, groups[0][1]):
-        total = total + gram_land[other]
+            back_round.send(back_raw.at[at], returned.at[2 * count + at - 1], (0, dy, dz))
+
+    rounds[-1].all_of_them().wait_recv()
+    total = added(gram_land, 0, groups[0][1])
     base = groups[0][1]
-    for members, count, shifts in groups[1:]:
-        me = base + place_in(members)
-        gram_land[me] = total
-        started = [sender.send(gram_land.at[me], gram_land.at[me], shift) for shift in shifts]
-        for copy in started:
-            copy.wait_recv()
-        total = gram_land[base]
-        for other in range(1, count):
-            total = total + gram_land[base + other]
-        base += count
+    for group in range(1, len(groups)):
+        rounds.append(gather_from(group, 0, gram_land, base, total))
+        rounds[-1].all_of_them().wait_recv()
+        total = added(gram_land, base, groups[group][1])
+        base += groups[group][1]
+    rounds.append(back_round)
     gram = jnp.concatenate([total[:, r : r + rows] for r in range(0, rows * rows // 8, rows)], axis=0) / entries
 
-    for copy in arriving:
-        copy.wait_recv()
-    own = back_raw[0]
-    low, up = low_back[0], up_back[0]
-    for at in range(1, len(planes)):
-        own = own + raw_back[at]
-        low = low + low_back[at]
-        up = up + up_back[at]
+    back_round.all_of_them().wait_recv()
+    own, up, low = back_raw[0], returned[0], returned[count]
+    for at in range(1, count):
+        own = own + returned[2 * count + at - 1]
+        up = up + returned[at]
+        low = low + returned[count + at]
     own = own + select_dot(jnp.where(early, up, low), pick_x, ((1,), (1,)))
     hv = jnp.concatenate([own[c : c + 1, :] for c in range(3)], axis=1)
     stack[stored : stored + 1, :] = hv
     sums = dot_full(jnp.broadcast_to(hv, (8, 3 * atoms)), stack[...], ((1,), (1,)))
-    sums = jnp.concatenate([sums[0:1], jnp.zeros((1, row_tile.shape[1] - rows), F32)], axis=1)
+    sums = jnp.concatenate([sums[0:1], jnp.zeros((1, row_land.shape[2] - rows), F32)], axis=1)
     base = 0
-    for members, count, shifts in groups:
-        me = base + place_in(members)
-        row_land[me] = sums
-        started = [sender.send(row_land.at[me], row_land.at[me], shift) for shift in shifts]
-        for copy in started:
-            copy.wait_recv()
-        sums = row_land[base]
-        for other in range(1, count):
-            sums = sums + row_land[base + other]
-        base += count
-    for copy in sender.started:
-        copy.wait_send()
-    assert sender.used == copies
+    for group in range(len(groups)):
+        rounds.append(gather_from(group, 1, row_land, base, sums))
+        rounds[-1].all_of_them().wait_recv()
+        sums = added(row_land, base, groups[group][1])
+        base += groups[group][1]
+    for around in rounds:
+        around.all_of_them().wait_send()
     lane = lax.broadcasted_iota(jnp.int32, (1, rows), 1)
     sums = sums[:, :rows] / entries
     kept = jnp.where(lane < stored, sums, 0.0)
@@ -683,13 +680,13 @@
     planes = len(plane_offsets())
     groups = reduction_groups()
     slots = sum(count for _, count, _ in groups)
-    copies = 2 * (3 * planes - 1) + 2 * sum(len(shifts) for _, _, shifts in groups)
     hvp = hvp_shapes(atoms, width, types, levels, m1, m2, fit_w2.shape[0], ext)
     any_space = pl.BlockSpec(memory_space=pl.ANY)
     vmem = pl.BlockSpec(memory_space=pltpu.VMEM)
-    tile = pltpu.VMEM((planes, 8, pair), F32)
+    tiles = pltpu.VMEM((planes, 8, pair), F32)
+    arrivals = pltpu.VMEM((3 * planes - 1, 8, pair), F32)
     next_vector, correlations, norm = pl.pallas_call(
-        functools.partial(lanczos_kernel, inputs=len(args), copies=copies, names=tuple(hvp)),
+        functools.partial(lanczos_kernel, inputs=len(args), names=tuple(hvp)),
         out_shape=(
             jax.ShapeDtypeStruct((3, 1, atoms), F32),
             jax.ShapeDtypeStruct((1, stored), F32),
@@ -699,17 +696,17 @@
         out_specs=(vmem,) * 3,
         scratch_shapes=[pltpu.VMEM(x.shape, x.dtype) for x in args] + [
             pltpu.SemaphoreType.DMA((len(args),)),
-            pltpu.SemaphoreType.DMA((copies,)),
-            pltpu.SemaphoreType.DMA((copies,)),
+            pltpu.SemaphoreType.DMA((2 + 2 * len(groups), 2)),
             pltpu.VMEM((8, ext), F32),
             pltpu.VMEM((8, ext), F32),
             pltpu.VMEM((8, pair), F32),
             pltpu.VMEM((8, pair), F32),
-            tile, tile, tile, tile, tile, tile, tile, tile,
+            arrivals,
+            tiles,
+            tiles,
+            arrivals,
             pltpu.VMEM((rows, 3 * atoms), F32),
-            pltpu.VMEM((8, rows * rows // 8), F32),
             pltpu.VMEM((slots, 8, rows * rows // 8), F32),
-            pltpu.VMEM((1, 128), F32),
             pltpu.VMEM((slots, 1, 128), F32),
         ] + [pltpu.VMEM(shape, dtype) for shape, dtype in hvp.values()],
         compiler_params=pltpu.CompilerParams(

time: 35.9 us -> 32.9 us (0.916)
  Pallas kernels: 30.9 us -> 28 us
    pallas_call x1, Pallas kernels: 30.9 us -> 28 us  [on_device(): pl.pallas_call(functools.partial(lanczos_kernel, inputs=len(args), names=...]
where the time goes in v5:
time: 32.9 us; the launch traced here: 32.7 us
  Pallas kernels  28 us (85%)
  between operations  2.41 us (7%)
  local copies, waits for them, and re-layouts  2.37 us (7%)
    pallas_call x1, Pallas kernels, on_device(): pl.pallas_call(functools.partial(lanczos_kernel, inputs=len(args), names=...  28 us
    unnamed x2, local copies, waits for them, and re-layouts  2.37 us

profile of v5, /device:TPU:0, one launch (start us, length us, event | category | flops | bytes accessed | tf_op | source)
XLA Modules:
  0.0 32.7 jit_solution(9141699481629901968)
XLA Ops:
  0.6 28.0 %lanczos.1 = (f32[3,1,128]{2,1,0:T(1,128)}, f32[1,30]{1,0:T(1,128)}, f32[1,1]{1,0:T(1,128)}) custom-call(f32[3,1,128]{2,1,0:T(1,128)} %bitcast.20, f32[30,3,1,128]{3,2,1,0:T(1,128)} %bitcast.19, s32[128,128]{1,0:T(8,128)} %bitcast.18, s32[1,128]{1,0:T(1,128)} %bitcast.28, s32[1,128]{1,0:T(1,128)} %bitcast.29, s32[2,64]{1,0:T(2,128)} %bitcast.22, ...), custom_call_target="tpu_custom_call" | custom-call | tf_op jit(solution)/shard_map/lanczos/pallas_call | solution.py:688
  28.6 1.2 %copy.21 = f32[3,1,1,1,128]{4,3,2,1,0:T(1,128)} copy(f32[3,1,1,1,128]{4,3,2,1,0:T(1,128)} %bitcast.21) | data formatting | bytes 3072
  29.8 1.1 %copy.22 = f32[30]{0:T(128)} copy(f32[30]{0:T(128)} %bitcast.30) | data formatting | bytes 240

commit v6 on v5

--- a/solution.py
+++ b/solution.py
@@ -651,6 +651,16 @@
         next_ref[c] = (hv[:, part] - mixed[:, rows:][:, part]) / norm
 
 
+def hand_over(*refs):
+    count = (len(refs) - 1) // 2
+    sems = refs[-1]
+    copies = [pltpu.make_async_copy(refs[at], refs[count + at], sems.at[at]) for at in range(count)]
+    for copy in copies:
+        copy.start()
+    for copy in copies:
+        copy.wait()
+
+
 def on_device(positions, basis, neighbours, used_count, kinds, map_x, map_y, map_z,
               table, fit_w1, fit_b1, fit_w2, fit_b2, fit_out):
     atoms = positions.shape[-1]
@@ -685,7 +695,7 @@
     vmem = pl.BlockSpec(memory_space=pltpu.VMEM)
     tiles = pltpu.VMEM((planes, 8, pair), F32)
     arrivals = pltpu.VMEM((3 * planes - 1, 8, pair), F32)
-    next_vector, correlations, norm = pl.pallas_call(
+    results = pl.pallas_call(
         functools.partial(lanczos_kernel, inputs=len(args), names=tuple(hvp)),
         out_shape=(
             jax.ShapeDtypeStruct((3, 1, atoms), F32),
@@ -714,6 +724,15 @@
         ),
         name="lanczos",
     )(*args)
+    results = pl.pallas_call(
+        hand_over,
+        out_shape=tuple(jax.ShapeDtypeStruct(x.shape, x.dtype) for x in results),
+        in_specs=[any_space] * 3,
+        out_specs=(any_space,) * 3,
+        scratch_shapes=[pltpu.SemaphoreType.DMA((3,))],
+        name="hand_over",
+    )(*results)
+    next_vector, correlations, norm = results
     return next_vector.reshape(positions.shape), correlations.reshape(stored), norm.reshape(())
 
 

time: 32.9 us -> 30.6 us (0.930)
  local copies, waits for them, and re-layouts: 2.37 us -> 0 us
  between operations: 2.41 us -> 0.64 us
  Pallas kernels: 28 us -> 29.7 us
    unnamed x2 -> x0, local copies, waits for them, and re-layouts: 2.37 us -> none
    pallas_call x0 -> x1, Pallas kernels: none -> 1.8 us  [on_device(): pl.pallas_call(hand_over, out_shape=tuple((jax.ShapeDtypeStruct(x.shape,...]
where the time goes in v6:
time: 30.6 us; the launch traced here: 30.4 us
  Pallas kernels  29.7 us (97%)
  between operations  0.64 us (2%)
    pallas_call x1, Pallas kernels, on_device(): pl.pallas_call(functools.partial(lanczos_kernel, inputs=len(args), names=...  27.9 us
    pallas_call x1, Pallas kernels, on_device(): pl.pallas_call(hand_over, out_shape=tuple((jax.ShapeDtypeStruct(x.shape,...  1.8 us

profile of v6, /device:TPU:0, one launch (start us, length us, event | category | flops | bytes accessed | tf_op | source)
XLA Modules:
  0.0 30.4 jit_solution(13929422991486727770)
XLA Ops:
  0.6 27.9 %lanczos.1 = (f32[3,1,128]{2,1,0:T(1,128)}, f32[1,30]{1,0:T(1,128)}, f32[1,1]{1,0:T(1,128)}) custom-call(f32[3,1,128]{2,1,0:T(1,128)} %bitcast.20, f32[30,3,1,128]{3,2,1,0:T(1,128)} %bitcast.19, s32[128,128]{1,0:T(8,128)} %bitcast.18, s32[1,128]{1,0:T(1,128)} %bitcast.27, s32[1,128]{1,0:T(1,128)} %bitcast.28, s32[2,64]{1,0:T(2,128)} %bitcast.21, ...), custom_call_target="tpu_custom_call" | custom-call | tf_op jit(solution)/shard_map/lanczos/pallas_call | solution.py:698
  28.6 1.8 %hand_over.1 = (f32[3,1,128]{2,1,0:T(1,128)}, f32[1,30]{1,0:T(1,128)}, f32[1,1]{1,0:T(1,128)}) custom-call(f32[3,1,128]{2,1,0:T(1,128)} %get-tuple-element.9.refs_0_, f32[1,30]{1,0:T(1,128)} %get-tuple-element.10.refs_1_, f32[1,1]{1,0:T(1,128)} %get-tuple-element.11.refs_2_), custom_call_target="tpu_custom_call" | custom-call | tf_op jit(solution)/shard_map/hand_over/pallas_call | solution.py:727

commit v7 on v6

--- a/solution.py
+++ b/solution.py
@@ -54,7 +54,7 @@
     return dict(
         idt=((width, atoms), jnp.int32),
         onehot=((width // CHUNK, DIGIT, CHUNK * atoms), BF16),
-        in_bank=((ext // DIGIT, width, atoms), F32),
+        in_bank=((width, ext // DIGIT, atoms), F32),
         w1_rows=((fit_wide // 128, m1_wide * m2, 128), F32),
         w1_low=((fit_wide // 128, types * low, 128), F32),
         low_right=((types * fit, 3 * low), BF16),
@@ -72,7 +72,7 @@
         product=((low, 2 * atoms), F32),
         pulled=((low, 2 * atoms), F32),
         gp=((levels, 8 * atoms), F32),
-        forces=((width * 8, atoms), F32),
+        forces=((6, width + CHUNK, atoms), F32),
     )
 
 
@@ -106,7 +106,6 @@
         first = table_ref[t][:, :m2]
         h.lead_down[t * levels : (t + 1) * levels, :] = left_parts(first)
         h.lead_up[t * m2 : (t + 1) * m2, :] = left_parts(dot_full(first, identity(levels), ((0,), (0,))))
-    h.forces[...] = jnp.zeros_like(h.forces)
 
 
 def identity(n):
@@ -117,14 +116,15 @@
 def prepare_scatter(h, ids_ref):
     width, atoms = h.idt.shape
     h.idt[...] = ids_ref[...].T
-    bank = jnp.right_shift(h.idt[...], DIGIT.bit_length() - 1)
-    for b in range(h.in_bank.shape[0]):
-        h.in_bank[b] = jnp.where(bank == b, 1.0, 0.0).astype(F32)
+    group = lax.broadcasted_iota(jnp.int32, h.in_bank.shape[1:], 0)
     column = lax.broadcasted_iota(jnp.int32, (DIGIT, atoms), 0)
 
     def one(c, carry):
-        digit = jnp.bitwise_and(h.idt[pl.ds(pl.multiple_of(c * CHUNK, CHUNK), CHUNK), :], DIGIT - 1)
+        idx = h.idt[pl.ds(pl.multiple_of(c * CHUNK, CHUNK), CHUNK), :]
+        digit = jnp.bitwise_and(idx, DIGIT - 1)
+        bank = jnp.right_shift(idx, DIGIT.bit_length() - 1)
         for r in range(CHUNK):
+            h.in_bank[c * CHUNK + r] = jnp.where(bank[r : r + 1, :] == group, 1.0, 0.0).astype(F32)
             hit = jnp.where(digit[r : r + 1, :] == column, 1.0, 0.0)
             h.onehot[c, :, r * atoms : (r + 1) * atoms] = hit.astype(BF16)
         return carry
@@ -282,7 +282,7 @@
 def pair_forces(h, out_ref):
     width, atoms = h.idt.shape
     levels = h.gauss.shape[0]
-    banks = h.in_bank.shape[0]
+    banks = h.in_bank.shape[1]
     top = float(levels - 1)
 
     def force_of(c, centre):
@@ -333,36 +333,41 @@
         for e in range(3):
             force = 2.0 * (v[e] * kern + d[e] * dkern) + du * val[1 + e] + u * dval[1 + e]
             high = force.astype(BF16).astype(F32)
-            h.forces[pl.ds(first * 8 + e, CHUNK, stride=8), :] = high
-            h.forces[pl.ds(first * 8 + 3 + e, CHUNK, stride=8), :] = force - high
+            h.forces[e, here, :] = high
+            h.forces[3 + e, here, :] = force - high
             out.append(centre[e] - force)
         return tuple(out)
 
     zero = jnp.zeros((CHUNK, atoms), F32)
-    centre = lax.fori_loop(0, width // CHUNK, force_of, (zero,) * 3)
-
-    together = width // 2
-
-    def scatter(c, acc):
+    def scatter(first, chunks):
         lefts = []
-        for r in range(together):
-            n = c * together + r
-            part = h.forces[pl.ds(pl.multiple_of(n * 8, 8), 8), :]
-            lefts.append(
-                jnp.concatenate([part * h.in_bank[b, pl.ds(n, 1), :] for b in range(banks)], axis=0).astype(BF16)
-            )
-        right = jnp.concatenate([h.onehot[c * (together // CHUNK) + j] for j in range(together // CHUNK)], axis=1)
-        return acc + lax.dot_general(
+        for n in range(first * CHUNK, (first + chunks) * CHUNK):
+            mine = h.in_bank[n]
+            lefts.append(jnp.concatenate([h.forces[e, n : n + 1, :] * mine for e in range(6)], axis=0).astype(BF16))
+        right = jnp.concatenate([h.onehot[first + j] for j in range(chunks)], axis=1)
+        return lax.dot_general(
             jnp.concatenate(lefts, axis=1), right, (((1,), (1,)), ((), ())), preferred_element_type=F32
         )
 
-    acc = lax.fori_loop(0, width // together, scatter, jnp.zeros((8 * banks, DIGIT), F32))
+    chunks = width // CHUNK
+    centre = (zero,) * 3
+    acc = None
+    for piece in range(4):
+        if piece:
+            part = scatter((piece - 1) * chunks // 4, chunks // 4)
+            acc = part if acc is None else acc + part
+        for c in range(piece * chunks // 4, (piece + 1) * chunks // 4):
+            centre = force_of(c, centre)
+    acc = acc + scatter(3 * chunks // 4, chunks // 4)
     per = 128 // DIGIT
-    for b in range(0, banks, per):
-        part = jnp.concatenate([acc[8 * j : 8 * j + 8] for j in range(b, b + per)], axis=1)
-        out_ref[:, b * DIGIT : (b + per) * DIGIT] = part + jnp.concatenate([part[3:], part[:3]], axis=0)
+    out_ref[3:, :] = jnp.zeros((out_ref.shape[0] - 3, out_ref.shape[1]), F32)
     for e in range(3):
-        out_ref[e : e + 1, :atoms] += jnp.sum(centre[e], axis=0, keepdims=True)
+        part = acc[banks * e : banks * (e + 1)] + acc[banks * (3 + e) : banks * (4 + e)]
+        for b in range(0, banks, per):
+            row = jnp.concatenate([part[j : j + 1] for j in range(b, b + per)], axis=1)
+            if b == 0:
+                row = row + jnp.sum(centre[e], axis=0, keepdims=True)
+            out_ref[e : e + 1, b * DIGIT : (b + per) * DIGIT] = row
 
 
 def hessian_product(h, ext_ref, counts_ref, kinds_ref, out_ref, types):
@@ -395,11 +400,18 @@
     return [(dy, dz) for dz in along(nz) for dy in along(ny)]
 
 
-def device_at(shift):
-    return {
-        axis: lax.rem(lax.axis_index(axis) + (step + peers) % peers, peers)
-        for axis, step, peers in zip(AXES, shift, sizes_of())
-    }
+class Grid:
+    def __init__(self):
+        self.sizes = sizes_of()
+        self.along = []
+        for axis, peers in zip(AXES, self.sizes):
+            me = lax.axis_index(axis)
+            self.along.append([me] + [lax.rem(me + step, peers) for step in range(1, peers)])
+
+    def device(self, shift):
+        return {
+            axis: row[step % peers] for axis, row, step, peers in zip(AXES, self.along, shift, self.sizes)
+        }
 
 
 def reduction_groups():
@@ -459,8 +471,8 @@
 
 
 class Round:
-    def __init__(self, sems, at, landed):
-        self.sems, self.at, self.landed = sems, at, landed
+    def __init__(self, grid, sems, at, landed):
+        self.grid, self.sems, self.at, self.landed = grid, sems, at, landed
 
     def copy(self, source, target, shift):
         return pltpu.make_async_remote_copy(
@@ -468,7 +480,7 @@
             dst_ref=target,
             send_sem=self.sems.at[self.at, 0],
             recv_sem=self.sems.at[self.at, 1],
-            device_id=device_at(shift),
+            device_id=self.grid.device(shift),
             device_id_type=MESH,
         )
 
@@ -483,7 +495,7 @@
 def lanczos_kernel(*refs, inputs, names):
     hbm, (next_ref, corr_ref, norm_ref) = refs[:inputs], refs[inputs : inputs + 3]
     local = refs[inputs + 3 : 2 * inputs + 3]
-    (load_sem, round_sem, ext, work, mine, face, landed, back_raw, back_face, returned, stack, gram_land, row_land, *hvp_scratch) = refs[2 * inputs + 3 :]
+    (load_sem, round_sem, ext, work, mine, face, landed, back_raw, back_face, returned, stack, mixed_right, gram_land, row_land, *hvp_scratch) = refs[2 * inputs + 3 :]
     places, basis, ids, counts, kinds, map_x, map_y, map_z, table, w1, w2, b1, b2, fo = local
     h = Scratch(names, hvp_scratch)
     types = table.shape[0]
@@ -491,7 +503,8 @@
     stored = basis.shape[0]
     rows = stack.shape[0]
     pair = 2 * map_x.shape[1]
-    sizes = sizes_of()
+    grid = Grid()
+    sizes = grid.sizes
     entries = 3 * atoms * sizes[0] * sizes[1] * sizes[2]
     planes = plane_offsets()
     groups = reduction_groups()
@@ -508,7 +521,7 @@
     assert opposite == set(partners)
     barrier = pltpu.get_barrier_semaphore()
     for shift in partners:
-        pl.semaphore_signal(barrier, inc=1, device_id=device_at(shift), device_id_type=MESH)
+        pl.semaphore_signal(barrier, inc=1, device_id=grid.device(shift), device_id_type=MESH)
     loads = [pltpu.make_async_copy(a, b, load_sem.at[at]) for at, (a, b) in enumerate(zip(hbm, local))]
     for at in (0, 1, 5, 6, 7, 2, 3, 4, 8, 9, 10, 11, 12, 13):
         loads[at].start()
@@ -526,7 +539,7 @@
     face[...] = select_dot(mine[...], pick_x, ((1,), (0,)))
     pl.semaphore_wait(barrier, len(partners))
 
-    halo = Round(round_sem, 0, landed)
+    halo = Round(grid, round_sem, 0, landed)
     for at, (dy, dz) in reversed(list(enumerate(planes))):
         halo.send(face, landed.at[at], (1, -dy, -dz))
         halo.send(face, landed.at[count + at], (-1, -dy, -dz))
@@ -573,16 +586,16 @@
         members, size, shifts = groups[group]
         me = base + place_in(members)
         tiles[me] = value
-        around = Round(round_sem, 2 + 2 * group + kind, tiles.at[pl.ds(base, size - 1)])
+        around = Round(grid, round_sem, 2 + 2 * group + kind, tiles.at[pl.ds(base, size - 1)])
         for shift in shifts:
             around.send(tiles.at[me], tiles.at[me], shift)
         return around
 
     def added(tiles, base, size):
-        total = tiles[base]
-        for other in range(1, size):
-            total = total + tiles[base + other]
-        return total
+        terms = [tiles[base + at] for at in range(size)]
+        while len(terms) > 1:
+            terms = [sum(terms[at : at + 2][1:], terms[at]) for at in range(0, len(terms), 2)]
+        return terms[0]
 
     rounds = [halo, gather_from(0, 0, gram_land, 0, gram)]
 
@@ -597,7 +610,7 @@
     for dy, dz in pick_y:
         part = one_side(back[dz][:, atoms + pair :], dy, many_y, early)
         terms[dy, dz] = select_dot(part, pick_y[dy, dz], ((1,), (1,)))
-    back_round = Round(round_sem, 1, returned)
+    back_round = Round(grid, round_sem, 1, returned)
     for at, (dy, dz) in reversed(list(enumerate(planes))):
         back_raw[at] = terms[dy, dz][:, :atoms]
         back_face[at] = terms[dy, dz][:, atoms:]
@@ -617,6 +630,9 @@
     rounds.append(back_round)
     gram = jnp.concatenate([total[:, r : r + rows] for r in range(0, rows * rows // 8, rows)], axis=0) / entries
 
+    high, low = split(stack[...])
+    stack_right = jnp.concatenate([high, high, low], axis=1)
+    mixed_right[...] = right_parts(jnp.concatenate([padded(gram, 0, 128), stack[...]], axis=1))
     back_round.all_of_them().wait_recv()
     own, up, low = back_raw[0], returned[0], returned[count]
     for at in range(1, count):
@@ -625,9 +641,12 @@
         low = low + returned[count + at]
     own = own + select_dot(jnp.where(early, up, low), pick_x, ((1,), (1,)))
     hv = jnp.concatenate([own[c : c + 1, :] for c in range(3)], axis=1)
-    stack[stored : stored + 1, :] = hv
-    sums = dot_full(jnp.broadcast_to(hv, (8, 3 * atoms)), stack[...], ((1,), (1,)))
+    sums = lax.dot_general(
+        left_parts(jnp.broadcast_to(hv, (8, 3 * atoms))), stack_right, (((1,), (1,)), ((), ())), preferred_element_type=F32
+    )
+    lane = lax.broadcasted_iota(jnp.int32, (1, row_land.shape[2]), 1)
     sums = jnp.concatenate([sums[0:1], jnp.zeros((1, row_land.shape[2] - rows), F32)], axis=1)
+    sums = jnp.where(lane == stored, jnp.sum(hv * hv, axis=1, keepdims=True), sums)
     base = 0
     for group in range(len(groups)):
         rounds.append(gather_from(group, 1, row_land, base, sums))
@@ -636,11 +655,9 @@
         base += groups[group][1]
     for around in rounds:
         around.all_of_them().wait_send()
-    lane = lax.broadcasted_iota(jnp.int32, (1, rows), 1)
     sums = sums[:, :rows] / entries
-    kept = jnp.where(lane < stored, sums, 0.0)
-    both = jnp.concatenate([gram, stack[...]], axis=1)
-    mixed = dot_full(jnp.broadcast_to(kept, (8, rows)), both, ((1,), (0,)))[0:1]
+    kept = jnp.where(lane[:, :rows] < stored, sums, 0.0)
+    mixed = matmul(left_parts(jnp.broadcast_to(kept, (8, rows))), mixed_right[...])[0:1]
     plain = sums[:, stored : stored + 1]
     cross = jnp.sum(mixed[:, :rows] * kept - 2.0 * kept * kept, axis=1, keepdims=True)
     norm = jnp.sqrt(plain + cross + 1e-06)
@@ -648,7 +665,7 @@
     corr_ref[...] = sums[:, :stored]
     for c in range(3):
         part = slice(c * atoms, (c + 1) * atoms)
-        next_ref[c] = (hv[:, part] - mixed[:, rows:][:, part]) / norm
+        next_ref[c] = (hv[:, part] - mixed[:, 128:][:, part]) / norm
 
 
 def hand_over(*refs):
@@ -716,6 +733,7 @@
             tiles,
             arrivals,
             pltpu.VMEM((rows, 3 * atoms), F32),
+            pltpu.VMEM((3 * rows, 128 + 3 * atoms), BF16),
             pltpu.VMEM((slots, 8, rows * rows // 8), F32),
             pltpu.VMEM((slots, 1, 128), F32),
         ] + [pltpu.VMEM(shape, dtype) for shape, dtype in hvp.values()],

time: 30.6 us -> 30.1 us (0.984)
  Pallas kernels: 29.7 us -> 29.3 us
    pallas_call x1, Pallas kernels: 27.9 us -> 27.5 us  [on_device(): pl.pallas_call(functools.partial(lanczos_kernel, inputs=len(args), names=...]
where the time goes in v7:
time: 30.1 us; the launch traced here: 29.9 us
  Pallas kernels  29.3 us (97%)
  between operations  0.64 us (2%)
    pallas_call x1, Pallas kernels, on_device(): pl.pallas_call(functools.partial(lanczos_kernel, inputs=len(args), names=...  27.5 us
    pallas_call x1, Pallas kernels, on_device(): pl.pallas_call(hand_over, out_shape=tuple((jax.ShapeDtypeStruct(x.shape,...  1.8 us

profile of v7, /device:TPU:0, one launch (start us, length us, event | category | flops | bytes accessed | tf_op | source)
XLA Modules:
  0.0 29.9 jit_solution(9134280443420979541)
XLA Ops:
  0.6 27.5 %lanczos.1 = (f32[3,1,128]{2,1,0:T(1,128)}, f32[1,30]{1,0:T(1,128)}, f32[1,1]{1,0:T(1,128)}) custom-call(f32[3,1,128]{2,1,0:T(1,128)} %bitcast.20, f32[30,3,1,128]{3,2,1,0:T(1,128)} %bitcast.19, s32[128,128]{1,0:T(8,128)} %bitcast.18, s32[1,128]{1,0:T(1,128)} %bitcast.27, s32[1,128]{1,0:T(1,128)} %bitcast.28, s32[2,64]{1,0:T(2,128)} %bitcast.21, ...), custom_call_target="tpu_custom_call" | custom-call | tf_op jit(solution)/shard_map/lanczos/pallas_call | solution.py:715
  28.1 1.8 %hand_over.1 = (f32[3,1,128]{2,1,0:T(1,128)}, f32[1,30]{1,0:T(1,128)}, f32[1,1]{1,0:T(1,128)}) custom-call(f32[3,1,128]{2,1,0:T(1,128)} %get-tuple-element.9.refs_0_, f32[1,30]{1,0:T(1,128)} %get-tuple-element.10.refs_1_, f32[1,1]{1,0:T(1,128)} %get-tuple-element.11.refs_2_), custom_call_target="tpu_custom_call" | custom-call | tf_op jit(solution)/shard_map/hand_over/pallas_call | solution.py:745

commit v8 on v7

--- a/solution.py
+++ b/solution.py
@@ -190,7 +190,7 @@
 def pooled_terms(h):
     width, atoms = h.idt.shape
     levels = h.gauss.shape[0]
-    together = 4
+    together = 2
     zero = jnp.zeros((CHUNK, atoms), F32)
     for k0 in range(0, levels, together):
 
@@ -370,13 +370,6 @@
             out_ref[e : e + 1, b * DIGIT : (b + per) * DIGIT] = row
 
 
-def hessian_product(h, ext_ref, counts_ref, kinds_ref, out_ref, types):
-    pair_terms(h, ext_ref, counts_ref[...])
-    pooled_terms(h)
-    fitting_net(h, kinds_ref, types)
-    pair_forces(h, out_ref)
-
-
 class Scratch:
     def __init__(self, names, refs):
         for name, ref in zip(names, refs, strict=True):
@@ -537,6 +530,7 @@
     mine[7:8, :] = map_rows[2]
     pick_x = chosen_columns(map_rows[0], atoms)
     face[...] = select_dot(mine[...], pick_x, ((1,), (0,)))
+    returned[...] = jnp.zeros_like(returned)
     pl.semaphore_wait(barrier, len(partners))
 
     halo = Round(grid, round_sem, 0, landed)
@@ -597,9 +591,11 @@
             terms = [sum(terms[at : at + 2][1:], terms[at]) for at in range(0, len(terms), 2)]
         return terms[0]
 
+    pair_terms(h, ext, counts[...])
     rounds = [halo, gather_from(0, 0, gram_land, 0, gram)]
-
-    hessian_product(h, ext, counts, kinds, work, types)
+    pooled_terms(h)
+    fitting_net(h, kinds, types)
+    pair_forces(h, work)
 
     many_y, many_z = -1 in {dy for dy, _ in planes}, -1 in wider
     back = {0: work[:, : atoms + 2 * pair]}
@@ -610,14 +606,15 @@
     for dy, dz in pick_y:
         part = one_side(back[dz][:, atoms + pair :], dy, many_y, early)
         terms[dy, dz] = select_dot(part, pick_y[dy, dz], ((1,), (1,)))
-    back_round = Round(grid, round_sem, 1, returned)
+    lead = pl.ds(0, 3)
+    back_round = Round(grid, round_sem, 1, returned.at[:, lead])
     for at, (dy, dz) in reversed(list(enumerate(planes))):
         back_raw[at] = terms[dy, dz][:, :atoms]
         back_face[at] = terms[dy, dz][:, atoms:]
-        back_round.send(back_face.at[at], returned.at[at], (-1, dy, dz))
-        back_round.send(back_face.at[at], returned.at[count + at], (1, dy, dz))
+        back_round.send(back_face.at[at, lead], returned.at[at, lead], (-1, dy, dz))
+        back_round.send(back_face.at[at, lead], returned.at[count + at, lead], (1, dy, dz))
         if at:
-            back_round.send(back_raw.at[at], returned.at[2 * count + at - 1], (0, dy, dz))
+            back_round.send(back_raw.at[at, lead], returned.at[2 * count + at - 1, lead], (0, dy, dz))
 
     rounds[-1].all_of_them().wait_recv()
     total = added(gram_land, 0, groups[0][1])

time: 30.1 us -> 30 us (level)
  no operation moved by 1% of the time
where the time goes in v8:
time: 30 us; the launch traced here: 29.9 us
  Pallas kernels  29.2 us (97%)
  between operations  0.64 us (2%)
    pallas_call x1, Pallas kernels, on_device(): pl.pallas_call(functools.partial(lanczos_kernel, inputs=len(args), names=...  27.4 us
    pallas_call x1, Pallas kernels, on_device(): pl.pallas_call(hand_over, out_shape=tuple((jax.ShapeDtypeStruct(x.shape,...  1.8 us

profile of v8, /device:TPU:0, one launch (start us, length us, event | category | flops | bytes accessed | tf_op | source)
XLA Modules:
  0.0 29.9 jit_solution(16544335281382276520)
XLA Ops:
  0.6 27.4 %lanczos.1 = (f32[3,1,128]{2,1,0:T(1,128)}, f32[1,30]{1,0:T(1,128)}, f32[1,1]{1,0:T(1,128)}) custom-call(f32[3,1,128]{2,1,0:T(1,128)} %bitcast.20, f32[30,3,1,128]{3,2,1,0:T(1,128)} %bitcast.19, s32[128,128]{1,0:T(8,128)} %bitcast.18, s32[1,128]{1,0:T(1,128)} %bitcast.27, s32[1,128]{1,0:T(1,128)} %bitcast.28, s32[2,64]{1,0:T(2,128)} %bitcast.21, ...), custom_call_target="tpu_custom_call" | custom-call | tf_op jit(solution)/shard_map/lanczos/pallas_call | solution.py:712
  28.1 1.8 %hand_over.1 = (f32[3,1,128]{2,1,0:T(1,128)}, f32[1,30]{1,0:T(1,128)}, f32[1,1]{1,0:T(1,128)}) custom-call(f32[3,1,128]{2,1,0:T(1,128)} %get-tuple-element.9.refs_0_, f32[1,30]{1,0:T(1,128)} %get-tuple-element.10.refs_1_, f32[1,1]{1,0:T(1,128)} %get-tuple-element.11.refs_2_), custom_call_target="tpu_custom_call" | custom-call | tf_op jit(solution)/shard_map/hand_over/pallas_call | solution.py:742

commit v9 on v8

--- a/solution.py
+++ b/solution.py
@@ -329,9 +329,10 @@
             + qd * (t_qq * flow + t_q * (val_t[0] * s_q + big_t * u_q) + val[0] * s_qq + big * u_qq)
         )
         du = u_q * qd
+        kern, dkern = 2.0 * kern, 2.0 * dkern
         out = []
         for e in range(3):
-            force = 2.0 * (v[e] * kern + d[e] * dkern) + du * val[1 + e] + u * dval[1 + e]
+            force = v[e] * kern + d[e] * dkern + du * val[1 + e] + u * dval[1 + e]
             high = force.astype(BF16).astype(F32)
             h.forces[e, here, :] = high
             h.forces[3 + e, here, :] = force - high
@@ -509,7 +510,7 @@
             partners.add(tuple(step % peers for step, peers in zip((dx, dy, dz), sizes)))
     for _, _, shifts in groups:
         partners.update(shifts)
-    partners = sorted(partners - {(0, 0, 0)})
+    partners = sorted(partners - {(0, 0, 0)}, key=lambda shift: (-sum(map(bool, shift[::2])), shift))
     opposite = {tuple(-step % peers for step, peers in zip(shift, sizes)) for shift in partners}
     assert opposite == set(partners)
     barrier = pltpu.get_barrier_semaphore()

time: 30 us -> 30 us (level)
  no operation moved by 1% of the time
where the time goes in v9:
time: 30 us; the launch traced here: 29.8 us
  Pallas kernels  29.2 us (97%)
  between operations  0.64 us (2%)
    pallas_call x1, Pallas kernels, on_device(): pl.pallas_call(functools.partial(lanczos_kernel, inputs=len(args), names=...  27.4 us
    pallas_call x1, Pallas kernels, on_device(): pl.pallas_call(hand_over, out_shape=tuple((jax.ShapeDtypeStruct(x.shape,...  1.8 us

profile of v9, /device:TPU:0, one launch (start us, length us, event | category | flops | bytes accessed | tf_op | source)
XLA Modules:
  0.0 29.8 jit_solution(11099989592419546246)
XLA Ops:
  0.6 27.4 %lanczos.1 = (f32[3,1,128]{2,1,0:T(1,128)}, f32[1,30]{1,0:T(1,128)}, f32[1,1]{1,0:T(1,128)}) custom-call(f32[3,1,128]{2,1,0:T(1,128)} %bitcast.20, f32[30,3,1,128]{3,2,1,0:T(1,128)} %bitcast.19, s32[128,128]{1,0:T(8,128)} %bitcast.18, s32[1,128]{1,0:T(1,128)} %bitcast.27, s32[1,128]{1,0:T(1,128)} %bitcast.28, s32[2,64]{1,0:T(2,128)} %bitcast.21, ...), custom_call_target="tpu_custom_call" | custom-call | tf_op jit(solution)/shard_map/lanczos/pallas_call | solution.py:713
  28.0 1.8 %hand_over.1 = (f32[3,1,128]{2,1,0:T(1,128)}, f32[1,30]{1,0:T(1,128)}, f32[1,1]{1,0:T(1,128)}) custom-call(f32[3,1,128]{2,1,0:T(1,128)} %get-tuple-element.9.refs_0_, f32[1,30]{1,0:T(1,128)} %get-tuple-element.10.refs_1_, f32[1,1]{1,0:T(1,128)} %get-tuple-element.11.refs_2_), custom_call_target="tpu_custom_call" | custom-call | tf_op jit(solution)/shard_map/hand_over/pallas_call | solution.py:743
